TPU v7x, 32 devices: a whole 2x2x4 slice. The times are simulated.
32 devices in a mesh: dp: 4 (over z), stage: 2 (over y), tp: 4 (over x, core).
Axes of the slice: x: 2, y: 2, z: 4, core: 2. Of those that a mesh axis runs over, the one named last changes fastest.
Arguments:
- act_in: bfloat16 [2, 128, 14, 14, 512], P('stage', ('dp', 'tp'))
- w_conv: bfloat16 [2, 3, 3, 512, 512], P('stage', None, None, None, 'tp')
- gamma_vec: float32 [2, 512], P('stage', 'tp')
- beta_vec: float32 [2, 512], P('stage', 'tp')
- z_grad: bfloat16 [2, 128, 14, 14, 512], P('stage', 'dp', None, None, 'tp')
Outputs:
- output 1: bfloat16 [2, 128, 14, 14, 512], P('stage', 'dp', None, None, 'tp')
- output 2: bfloat16 [2, 128, 14, 14, 512], P('stage', ('dp', 'tp'))
- output 3: float32 [2, 3, 3, 512, 512], P('stage', None, None, None, 'tp')
All inputs are finite; a program needn't handle non-finite values.
Results may differ from a plain program's by a relative error of at most 0.00522.
Values are sent between devices in bfloat16 or wider.
A program may use at most 1 GiB of HBM per device.

v0:
```python
import jax
import jax.numpy as jnp
from jax import lax
from jax.sharding import PartitionSpec as P


def conv_fwd(images, kernel):
    return lax.conv_general_dilated(images, kernel, (1, 1), 'SAME', dimension_numbers=('NHWC', 'HWIO', 'NHWC'), preferred_element_type=jnp.float32)


def conv_input_grad(grad_map, kernel):
    flipped = lax.rev(kernel, (0, 1))
    return lax.conv_general_dilated(grad_map, flipped, (1, 1), 'SAME', dimension_numbers=('NHWC', 'HWOI', 'NHWC'), preferred_element_type=jnp.float32)


def conv_kernel_grad(images, grad_map):
    return lax.conv_general_dilated(images, grad_map, (1, 1), ((1, 1), (1, 1)), dimension_numbers=('CHWN', 'IHWO', 'HWNC'), preferred_element_type=jnp.float32)


def solution(mesh):
    act_spec = P('stage', ('dp', 'tp'))
    w_spec = P('stage', None, None, None, 'tp')
    vec_spec = P('stage', 'tp')
    chan_spec = P('stage', 'dp', None, None, 'tp')

    def device_step(act_in, w_conv, gamma_vec, beta_vec, z_grad):
        on_conv = lax.axis_index('stage') == 1
        arrived = lax.ppermute(act_in[0], 'stage', perm=[(0, 1)])
        group_act = lax.all_gather(arrived, 'tp', axis=0, tiled=True)
        kernel = w_conv[0]
        gamma_row = gamma_vec[0]
        beta_row = beta_vec[0]
        pre_act = conv_fwd(group_act, kernel)
        affine = pre_act * gamma_row + beta_row
        z_local = jnp.maximum(affine, 0.0).astype(jnp.bfloat16)
        grad_pre = jnp.where(affine > 0, z_grad[0] * gamma_row, 0.0).astype(jnp.bfloat16)
        act_part = conv_input_grad(grad_pre, kernel)
        act_mine = lax.psum_scatter(act_part, 'tp', scatter_dimension=0, tiled=True).astype(jnp.bfloat16)
        act_back = lax.ppermute(act_mine, 'stage', perm=[(1, 0)])
        w_part = conv_kernel_grad(group_act, grad_pre)
        w_total = lax.psum(w_part, 'dp')
        z_keep = jnp.where(on_conv, z_local, jnp.zeros_like(z_local))
        w_keep = jnp.where(on_conv, w_total, jnp.zeros_like(w_total))
        return z_keep[None], act_back[None], w_keep[None]

    return jax.shard_map(device_step, mesh=mesh, in_specs=(act_spec, w_spec, vec_spec, vec_spec, chan_spec), out_specs=(chan_spec, act_spec, w_spec), check_vma=False)
```

profile of v0, /device:TPU:4, one launch (start us, length us, event | category | flops | bytes accessed | tf_op | source)
XLA Modules:
  0.0 334.2 jit_solution(5237492157162068447)
XLA Ops:
  7.2 0.0 copy-start
  7.2 0.0 all-gather.2.cloned.1.call-start
  7.2 1.4 collective-permute-start
  8.7 37.4 %collective-permute-done = bf16[8,14,14,512]{3,0,2,1:T(8,128)(2,1)S(1)} collective-permute-done((bf16[8,14,14,512]{3,0,2,1:T(8,128)(2,1)}, bf16[8,14,14,512]{3,0,2,1:T(8,128)(2,1)S(1)}, u32[]{:S(2)}, u32[]{:S(2)}) %collective-permute-start) | collective-permute-done | bytes 1605664 | tf_op jit(solution)/shard_map/ppermute | solution.py:28
  46.1 1.2 copy-done.1
  47.2 0.0 all-gather.2.cloned.1.call-update
  47.3 0.0 reduce-scatter.2.cloned.1.call-start
  47.3 48.5 %all-gather.2.cloned.1.call-done = bf16[32,14,14,512]{3,0,2,1:T(8,128)(2,1)} async-done(((bf16[8,14,14,512]{3,0,2,1:T(8,128)(2,1)}), bf16[32,14,14,512]{3,0,2,1:T(8,128)(2,1)}) %all-gather.2.cloned.1.call-update) | async-done | bytes 6422544 | tf_op jit(solution)/shard_map/all_gather | solution.py:29
  95.8 0.0 copy-done
  95.8 19.2 %fusion.4 = (u16[32,14,128]{2,0,1:T(8,128)(2,1)S(1)}, f32[32,14,14,128]{3,0,2,1:T(8,128)}) fusion(f32[128]{0:T(128)} %bitcast.22, f32[128]{0:T(128)} %bitcast.24, bf16[32,14,14,512]{3,0,2,1:T(8,128)(2,1)} %all-gather.2.cloned.1.call-done, bf16[1,3,3,512,128]{4,3,2,1,0:T(8,128)(2,1)S(1)} %copy-done), kind=kOutput, calls=%fused_computation.10 | convolution fusion | flops 6716448768 | bytes 10929152 | tf_op jit(solution)/shard_map/conv_general_dilated | solution.py:8
  115.0 0.0 copy-done.3
  115.0 11.7 %fusion.5 = f32[32,14,14,512]{3,0,2,1:T(8,128)} fusion(bf16[1,3,3,512,128]{4,3,2,1,0:T(8,128)(2,1)S(1)} %copy-done, bf16[1,32,14,14,128]{4,1,3,2,0:T(8,128)(2,1)S(1)} %copy-done.4, f32[128]{0:T(128)S(1)} %bitcast.25, u16[32,14,128]{2,0,1:T(8,128)(2,1)S(1)} %get-tuple-element.3), kind=kOutput, calls=%fused_computation.11 | convolution fusion | flops 6717308928 | bytes 15745536 | tf_op jit(solution)/shard_map/conv_general_dilated | solution.py:13
  126.7 0.0 reduce-scatter.2.cloned.1.call-update
  126.7 0.2 all-reduce.2.cloned.1.call-start
  127.0 18.9 %fusion.9 = f32[3,3,512,128]{3,2,1,0:T(8,128)} fusion(bf16[32,14,14,512]{3,0,2,1:T(8,128)(2,1)} %all-gather.2.cloned.1.call-done, bf16[1,32,14,14,128]{4,1,3,2,0:T(8,128)(2,1)S(1)} %copy-done.4, f32[128]{0:T(128)S(1)} %bitcast.26, u16[32,14,128]{2,0,1:T(8,128)(2,1)S(1)} %get-tuple-element.3), kind=kOutput, calls=%fused_computation.15 | convolution fusion | flops 6717308928 | bytes 10502656 | tf_op jit(solution)/shard_map/conv_general_dilated | solution.py:17
  145.9 0.0 all-reduce.2.cloned.1.call-update
  145.9 78.6 %reduce-scatter.2.cloned.1.call-done = f32[8,14,14,512]{3,0,2,1:T(8,128)} async-done(((f32[32,14,14,512]{3,0,2,1:T(8,128)}), f32[8,14,14,512]{3,0,2,1:T(8,128)}) %reduce-scatter.2.cloned.1.call-update) | async-done | bytes 3211280 | tf_op jit(solution)/shard_map/reduce_scatter | solution.py:38
  224.6 2.2 convert_element_type.19
  226.7 3.6 %collective-permute-start.1 = (bf16[8,14,14,512]{3,0,2,1:T(8,128)(2,1)S(1)}, bf16[8,14,14,512]{3,0,2,1:T(8,128)(2,1)}, u32[]{:S(2)}, u32[]{:S(2)}) collective-permute-start(bf16[8,14,14,512]{3,0,2,1:T(8,128)(2,1)S(1)} %convert_element_type.19), channel_id=1, source_target_pairs={{4,0},{5,1},{6,2},{7,3},{12,8},{13,9},{14,10},{15,11},{20,16},{21,... | collective-permute-start | bytes 4816904 | tf_op jit(solution)/shard_map/ppermute | solution.py:39
  230.3 3.6 %fusion.3 = bf16[1,32,14,14,128]{4,1,3,2,0:T(8,128)(2,1)} fusion(f32[32,14,14,128]{3,0,2,1:T(8,128)} %get-tuple-element.4, f32[128]{0:T(128)S(1)} %bitcast.23, f32[128]{0:T(128)S(1)} %bitcast.27, pred[]{:T(512)S(6)} %eq.3), kind=kLoop, calls=%fused_computation.9 | loop fusion | flops 4014080 | bytes 4817921 | tf_op jit(solution)/shard_map/broadcast_in_dim | solution.py:44
  234.0 87.8 %all-reduce.2.cloned.1.call-done = f32[3,3,512,128]{3,2,1,0:T(8,128)} async-done(((f32[3,3,512,128]{3,2,1,0:T(8,128)}), f32[3,3,512,128]{3,2,1,0:T(8,128)}) %all-reduce.2.cloned.1.call-update) | async-done | bytes 2359312 | tf_op jit(solution)/shard_map/psum | solution.py:41
  321.7 3.2 select_bitcast_fusion
  325.0 0.0 collective-permute-done.1
  325.0 2.7 copy.10
  (6 shorter events, 0.0 us)
Async XLA Ops:
  7.2 88.6 %copy-start = (bf16[1,3,3,512,128]{4,3,2,1,0:T(8,128)(2,1)S(1)}, bf16[1,3,3,512,128]{4,3,2,1,0:T(8,128)(2,1)}, u32[]{:S(2)}) copy-start(bf16[1,3,3,512,128]{4,3,2,1,0:T(8,128)(2,1)} %param.6) | copy-start | bytes 3538948
  7.2 88.6 %all-gather.2.cloned.1.call-start = ((), (), s32[]{:S(2)}) async-start(), calls=%async_computation.1 | async-start | bytes 8028160 | tf_op jit(solution)/shard_map/all_gather | solution.py:29
  7.2 38.9 %collective-permute-start = (bf16[8,14,14,512]{3,0,2,1:T(8,128)(2,1)}, bf16[8,14,14,512]{3,0,2,1:T(8,128)(2,1)S(1)}, u32[]{:S(2)}, u32[]{:S(2)}) collective-permute-start(bf16[8,14,14,512]{3,0,2,1:T(8,128)(2,1)} %bitcast.28), channel_id=1, source_target_pairs={{0,4},{1,5},{2,6},{3,7},{8,12},{9,13},{10,14},{11,15},{16,20},{17,... | collective-permute-start | bytes 4816904 | tf_op jit(solution)/shard_map/ppermute | solution.py:28
  46.1 1.2 copy-start.1
  47.3 177.3 %reduce-scatter.2.cloned.1.call-start = ((), (), s32[]{:S(2)}) async-start(), calls=%async_computation.2 | async-start | bytes 16056320 | tf_op jit(solution)/shard_map/reduce_scatter | solution.py:38
  95.8 19.3 %copy-start.3 = (f32[1,128]{1,0:T(1,128)S(1)}, f32[1,128]{1,0:T(1,128)}, u32[]{:S(2)}) copy-start(f32[1,128]{1,0:T(1,128)} %param.7) | copy-start | bytes 1540
  95.8 19.3 %copy-start.4 = (bf16[1,32,14,14,128]{4,1,3,2,0:T(8,128)(2,1)S(1)}, bf16[1,32,14,14,128]{4,1,3,2,0:T(8,128)(2,1)}, u32[]{:S(2)}) copy-start(bf16[1,32,14,14,128]{4,1,3,2,0:T(8,128)(2,1)} %param.9) | copy-start | bytes 4816900
  126.7 195.0 %all-reduce.2.cloned.1.call-start = ((), (), s32[]{:S(2)}) async-start(), calls=%async_computation.3 | async-start | bytes 4718592 | tf_op jit(solution)/shard_map/psum | solution.py:41
  145.9 84.5 %copy-start.2 = (f32[1,128]{1,0:T(1,128)S(1)}, f32[1,128]{1,0:T(1,128)}, u32[]{:S(2)}) copy-start(f32[1,128]{1,0:T(1,128)} %param.8) | copy-start | bytes 1540
  226.7 98.3 %collective-permute-start.1 = (bf16[8,14,14,512]{3,0,2,1:T(8,128)(2,1)S(1)}, bf16[8,14,14,512]{3,0,2,1:T(8,128)(2,1)}, u32[]{:S(2)}, u32[]{:S(2)}) collective-permute-start(bf16[8,14,14,512]{3,0,2,1:T(8,128)(2,1)S(1)} %convert_element_type.19), channel_id=1, source_target_pairs={{4,0},{5,1},{6,2},{7,3},{12,8},{13,9},{14,10},{15,11},{20,16},{21,... | collective-permute-start | bytes 4816904 | tf_op jit(solution)/shard_map/ppermute | solution.py:39
Sparse Core Ops, SparseCore 0:
  47.4 48.3 all-gather.1
  126.9 97.6 reduce-scatter.1
  227.5 94.1 all-reduce.1
where the time goes:
time: 334 us
  waiting for transfers between devices  252 us (75%)
  matrix products  49.8 us (15%)
  between operations  13.8 us (4%)
  other arithmetic  9 us (3%)
  starting transfers between devices  5.34 us (2%)
  local copies, waits for them, and re-layouts  3.85 us (1%)
    psum x1, waiting for transfers between devices, device_step(): w_total = lax.psum(w_part, 'dp')  87.8 us
    reduce_scatter x1, waiting for transfers between devices, device_step(): lax.psum_scatter(act_part, 'tp', scatter_dimension=0, tiled=True)  78.6 us
    all_gather x1, waiting for transfers between devices, device_step(): group_act = lax.all_gather(arrived, 'tp', axis=0, tiled=True)  48.5 us
    ppermute x1, waiting for transfers between devices, device_step(): arrived = lax.ppermute(act_in[0], 'stage', perm=[(0, 1)])  37.4 us
    conv_general_dilated x1, matrix products, conv_fwd(): lax.conv_general_dilated(images, kernel, (1, 1), 'SAME', dimension_number...  19.2 us
    conv_general_dilated x1, matrix products, conv_kernel_grad(): lax.conv_general_dilated(images, grad_map, (1, 1), ((1, 1), (1, 1)), dime...  18.9 us
    conv_general_dilated x1, matrix products, conv_input_grad(): lax.conv_general_dilated(grad_map, flipped, (1, 1), 'SAME', dimension_num...  11.7 us
    broadcast_in_dim x2, other arithmetic, device_step(): return (z_keep[None], act_back[None], w_keep[None])  6.85 us
  transfers between devices with their start and end apart: 5, of which 4 were waited for; matrix products, arithmetic and copies ran while one was open for 8% of the time, Pallas kernels for 0%

commit v1 on v0

v1 whole, which is shorter than its diff:
```python
import functools

import jax
import jax.numpy as jnp
from jax import lax
from jax.experimental import pallas as pl
from jax.experimental.pallas import tpu as pltpu
from jax.sharding import PartitionSpec as P

MESH = pl.DeviceIdType.MESH
F32 = jnp.float32
BF16 = jnp.bfloat16
PAD = 16


def remote(src, dst, send_sem, recv_sem, dev):
    return pltpu.make_async_remote_copy(src_ref=src, dst_ref=dst, send_sem=send_sem, recv_sem=recv_sem, device_id=dev, device_id_type=MESH)


def block_kernel(H, WD, CI, CO, n_chunk, x_ref, w_ref, gam_ref, bet_ref, dz_ref, z_ref, dx_ref, dw_ref,
                 xe, xo, ge, go, wall, dzb, zb, vec, acc, prx, pb, rb, mb, xt, relay, dxb, *sems):
    (s_xs, s_xr, s_xf, s_gs, s_gr, s_gl, s_gf, s_wl, s_ws, s_wr, s_vl, s_vs, s_vr, s_dl, s_ds, s_dr,
     s_zl, s_zs, s_zr, s_ps, s_pr, s_os, s_or, s_ms, s_mr, s_ts, s_tr, s_tl, s_dx) = sems
    R = WD * 8
    CW = 2 * CO
    zi = lax.axis_index("dp")
    st = lax.axis_index("stage")
    tp = lax.axis_index("tp")
    xi = tp // 2
    c = tp % 2
    y_dev = (zi, 1 - st, tp)
    x_dev = (zi, st, 2 * (1 - xi) + c)
    c_dev = (zi, st, 2 * xi + 1 - c)
    z_mate = jnp.where(zi == 1, 2, 1)
    z_out = jnp.where(zi < 2, 0, 3)
    z_in = jnp.where(zi < 2, 1, 2)
    inner = jnp.logical_or(zi == 1, zi == 2)
    mate_dev = (z_mate, st, tp)
    outer_dev = (z_out, st, tp)
    inner_dev = (z_in, st, tp)

    barrier = pltpu.get_barrier_semaphore()
    for dev in (y_dev, x_dev, c_dev):
        pl.semaphore_signal(barrier, inc=1, device_id=dev, device_id_type=MESH)

    @pl.when(inner)
    def _():
        for dev in (mate_dev, outer_dev):
            pl.semaphore_signal(barrier, inc=1, device_id=dev, device_id_type=MESH)
        pl.semaphore_wait(barrier, 5)

    @pl.when(jnp.logical_not(inner))
    def _():
        pl.semaphore_signal(barrier, inc=1, device_id=inner_dev, device_id_type=MESH)
        pl.semaphore_wait(barrier, 4)

    def zero_borders(buf):
        ch = buf.shape[-1]

        def rows(h, _):
            for s in range(2):
                buf[s, h, 0:PAD, :] = jnp.zeros((PAD, ch), BF16)
                buf[s, h, PAD + R:, :] = jnp.zeros((buf.shape[2] - PAD - R, ch), BF16)
            return 0

        lax.fori_loop(0, H + 2, rows, 0)

    def zero_planes(buf):
        for s in range(2):
            for h in (0, H + 1):
                buf[s, h] = jnp.zeros(buf.shape[2:], BF16)

    def odd_copy(even, odd, s, h):
        n = odd.shape[2]
        odd[s, h] = even[s, h, 8:8 + n, :]

    def tap_rows(even, odd, s, plane, shift, n):
        if shift == 0:
            return even[s, plane, PAD:PAD + n, :]
        start = PAD + 8 * shift - 8
        return odd[s, plane, start:start + n, :]

    @pl.when(st == 0)
    def _():
        def x_copy(h):
            return remote(x_ref.at[h], xe.at[xi, h + 1, pl.ds(PAD, R), :], s_xs.at[h], s_xr.at[xi, h], y_dev)

        lax.fori_loop(0, H, lambda h, _: (x_copy(h).start(), 0)[1], 0)
        zero_borders(ge)
        zero_planes(ge)
        zero_planes(go)

        def w_in(t, b):
            return remote(wall.at[b, t], wall.at[b, t], s_ws.at[0, t], s_wr.at[b, t], y_dev)

        def w_fwd(t, b, k, dev):
            return remote(wall.at[b, t], wall.at[b, t], s_ws.at[k, t], s_wr.at[b, t], dev)

        b_x = 2 * (1 - xi) + c

        def w_step(t, _):
            w_in(t, tp).wait_recv()
            w_fwd(t, tp, 0, c_dev).start()
            w_fwd(t, tp, 1, x_dev).start()
            return 0

        lax.fori_loop(0, 9, w_step, 0)

        def w_step2(t, _):
            w_in(t, b_x).wait_recv()
            w_fwd(t, b_x, 2, c_dev).start()
            return 0

        lax.fori_loop(0, 9, w_step2, 0)

        def w_step3(t, _):
            w_in(t, 2 * xi + 1 - c).wait_recv()
            w_in(t, 2 * (1 - xi) + 1 - c).wait_recv()
            return 0

        lax.fori_loop(0, 9, w_step3, 0)

        def g_in(j, b):
            return remote(ge.at[b, j + 1, pl.ds(PAD, R), :], ge.at[b, j + 1, pl.ds(PAD, R), :], s_gf.at[j], s_gr.at[b, j], y_dev)

        def relay_in(j):
            return remote(relay.at[j], relay.at[j], s_gf.at[j], s_gl.at[j], y_dev)

        def relay_out(j):
            return remote(relay.at[j], ge.at[xi, j + 1, pl.ds(PAD, R), :], s_gf.at[j], s_gr.at[xi, j], x_dev)

        def dx_out(h):
            return pltpu.make_async_copy(dxb.at[h], dx_ref.at[h], s_dx.at[h])

        def g_step(j, _):
            @pl.when(j < H)
            def _():
                relay_in(j).wait_recv()
                relay_out(j).start()
                g_in(j, xi).wait_recv()
                g_in(j, 1 - xi).wait_recv()
                for b in range(2):
                    odd_copy(ge, go, b, j + 1)

            @pl.when(j >= 1)
            def _():
                h = j - 1
                tot = jnp.zeros((R, CI), F32)
                for b in range(2):
                    for ky in range(3):
                        for kx in range(3):
                            t = 3 * ky + kx
                            lhs = tap_rows(ge, go, b, h + 2 - ky, 1 - kx, R)
                            rhs = jnp.concatenate([wall[2 * b, t], wall[2 * b + 1, t]], axis=1)
                            tot = tot + lax.dot_general(lhs, rhs, (((1,), (1,)), ((), ())), preferred_element_type=F32)
                dxb[h] = tot.astype(BF16)
                dx_out(h).start()

            return 0

        lax.fori_loop(0, H + 1, g_step, 0)

        def drain(h, _):
            x_copy(h).wait_send()
            relay_out(h).wait_send()
            dx_out(h).wait()
            return 0

        lax.fori_loop(0, H, drain, 0)

        def drain_w(t, _):
            w_fwd(t, tp, 0, c_dev).wait_send()
            w_fwd(t, tp, 1, x_dev).wait_send()
            w_fwd(t, b_x, 2, c_dev).wait_send()
            return 0

        lax.fori_loop(0, 9, drain_w, 0)

    @pl.when(st == 1)
    def _():
        w_loc = pltpu.make_async_copy(w_ref, wall.at[c], s_wl)
        w_core = remote(w_ref, wall.at[c], s_vs.at[2], s_vr.at[2], c_dev)
        vecs_l = [pltpu.make_async_copy(r, vec.at[k, c], s_vl.at[k]) for k, r in enumerate((gam_ref, bet_ref))]
        vecs_r = [remote(r, vec.at[k, c], s_vs.at[k], s_vr.at[k], c_dev) for k, r in enumerate((gam_ref, bet_ref))]
        dz_l = [pltpu.make_async_copy(dz_ref.at[:, :, 2 * s + c], dzb.at[s, c], s_dl.at[s]) for s in range(2)]
        dz_r = [remote(dz_ref.at[:, :, 2 * s + 1 - c], dzb.at[s, c], s_ds.at[s], s_dr.at[s], c_dev) for s in range(2)]

        def w_y(t):
            return remote(w_ref.at[t], wall.at[tp, t], s_ws.at[0, t], s_wr.at[tp, t], y_dev)

        w_loc.start()
        w_core.start()
        for k in range(2):
            vecs_l[k].start()
            vecs_r[k].start()
            dz_l[k].start()
            dz_r[k].start()
        lax.fori_loop(0, 9, lambda t, _: (w_y(t).start(), 0)[1], 0)

        zero_borders(xe)
        zero_borders(ge)
        for buf in (xe, xo, ge, go):
            zero_planes(buf)

        def zero_acc(t, _):
            for k in range(2):
                acc[k, t] = jnp.zeros((CI, CO), F32)
            return 0

        lax.fori_loop(0, 9, zero_acc, 0)
        for k in range(2):
            vecs_l[k].wait()
            vecs_r[k].wait_recv()
            dz_l[k].wait()
            dz_r[k].wait_recv()
        w_loc.wait()
        w_core.wait_recv()

        def x_in(j, s):
            view = xe.at[s, j + 1, pl.ds(PAD, R), :]
            return remote(view, view, s_xf.at[j], s_xr.at[s, j], y_dev)

        def x_fwd(j):
            view = xe.at[xi, j + 1, pl.ds(PAD, R), :]
            return remote(view, view, s_xf.at[j], s_xr.at[xi, j], x_dev)

        def g_own(h):
            return remote(ge.at[xi, h + 1, pl.ds(PAD, R), :], ge.at[xi, h + 1, pl.ds(PAD, R), :], s_gs.at[0, h], s_gr.at[xi, h], y_dev)

        def g_other(h):
            return remote(ge.at[1 - xi, h + 1, pl.ds(PAD, R), :], relay.at[h], s_gs.at[1, h], s_gl.at[h], y_dev)

        def step(j, _):
            @pl.when(j < H)
            def _():
                x_in(j, xi).wait_recv()
                x_fwd(j).start()
                x_in(j, 1 - xi).wait_recv()
                for s in range(2):
                    odd_copy(xe, xo, s, j + 1)

            @pl.when(jnp.logical_and(j >= 1, j < H + 1))
            def _():
                h = j - 1
                pre = jnp.zeros((2 * R, CW), F32)
                for ky in range(3):
                    for kx in range(3):
                        t = 3 * ky + kx
                        lhs = jnp.concatenate([tap_rows(xe, xo, s, h + ky, kx - 1, R) for s in range(2)], axis=0)
                        rhs = jnp.concatenate([wall[0, t], wall[1, t]], axis=1)
                        pre = pre + jnp.dot(lhs, rhs, preferred_element_type=F32)
                for k in range(2):
                    gam = vec[0, k]
                    bet = vec[1, k]
                    for s in range(2):
                        y = pre[s * R:(s + 1) * R, k * CO:(k + 1) * CO] * gam + bet
                        zb[s, k, h] = jnp.maximum(y, 0.0).reshape(WD, 8, CO).astype(BF16)
                        dzr = dzb[s, k, h].astype(F32).reshape(R, CO)
                        ge[s, h + 1, PAD:PAD + R, k * CO:(k + 1) * CO] = jnp.where(y > 0, dzr * gam, 0.0).astype(BF16)
                g_own(h).start()
                g_other(h).start()
                for s in range(2):
                    odd_copy(ge, go, s, h + 1)

            @pl.when(j >= 2)
            def _():
                q = j - 2
                rows = jnp.concatenate([xe[s, q + 1, PAD:PAD + 128, :] for s in range(2)], axis=0)
                xt[...] = rows.T
                for ky in range(3):
                    for kx in range(3):
                        t = 3 * ky + kx
                        rhs = jnp.concatenate([tap_rows(ge, go, s, q + 2 - ky, 1 - kx, 128) for s in range(2)], axis=0)
                        part = jnp.dot(xt[...], rhs, preferred_element_type=F32)
                        for k in range(2):
                            acc[k, t] += part[:, k * CO:(k + 1) * CO]

            return 0

        lax.fori_loop(0, H + 2, step, 0)

        def pair(t):
            return remote(acc.at[1 - c, t], prx.at[t], s_ps.at[t], s_pr.at[t], c_dev)

        lax.fori_loop(0, 9, lambda t, _: (pair(t).start(), 0)[1], 0)
        z_l = [pltpu.make_async_copy(zb.at[s, c], z_ref.at[:, :, 2 * s + c], s_zl.at[s]) for s in range(2)]
        z_r = [remote(zb.at[s, 1 - c], z_ref.at[:, :, 2 * s + c], s_zs.at[s], s_zr.at[s], c_dev) for s in range(2)]
        z_w = [remote(zb.at[s, 1 - c], z_ref.at[:, :, 2 * s + 1 - c], s_zs.at[s], s_zr.at[s], c_dev) for s in range(2)]
        for s in range(2):
            z_l[s].start()
            z_r[s].start()

        half = CI // 2

        def own_part(k):
            t = k // 2
            q = pl.multiple_of((k % 2) * half, half)

            @pl.when(k % 2 == 0)
            def _():
                pair(t).wait_recv()

            return acc[c, t, pl.ds(q, half), :] + prx[t, pl.ds(q, half), :]

        def dw_view(k):
            return dw_ref.at[k // 2, pl.ds(pl.multiple_of((k % 2) * half, half), half), :]

        def to_inner(k):
            return remote(pb.at[k], rb.at[k], s_os.at[k], s_or.at[k], inner_dev)

        def from_outer(k):
            return remote(pb.at[k], rb.at[k], s_os.at[k], s_or.at[k], outer_dev)

        def to_mate(k):
            return remote(pb.at[k], mb.at[k], s_ms.at[k], s_mr.at[k], mate_dev)

        def to_outer(k):
            return remote(rb.at[k], dw_view(k), s_ts.at[k], s_tr.at[k], outer_dev)

        def from_inner(k):
            return remote(rb.at[k], dw_view(k), s_ts.at[k], s_tr.at[k], inner_dev)

        def own_out(k):
            return pltpu.make_async_copy(rb.at[k], dw_view(k), s_tl.at[k])

        @pl.when(jnp.logical_not(inner))
        def _():
            def send(k, _):
                pb[k] = own_part(k)
                to_inner(k).start()
                return 0

            lax.fori_loop(0, n_chunk, send, 0)

            def take(k, _):
                from_inner(k).wait_recv()
                to_inner(k).wait_send()
                return 0

            lax.fori_loop(0, n_chunk, take, 0)

        @pl.when(inner)
        def _():
            LAG = 2

            def both(k, _):
                @pl.when(k < n_chunk)
                def _():
                    part = own_part(k)
                    from_outer(k).wait_recv()
                    pb[k] = part + rb[k]
                    to_mate(k).start()

                @pl.when(k >= LAG)
                def _():
                    m = k - LAG
                    to_mate(m).wait_recv()
                    rb[m] = pb[m] + mb[m]
                    to_outer(m).start()
                    own_out(m).start()

                return 0

            lax.fori_loop(0, n_chunk + LAG, both, 0)

            def done(k, _):
                to_mate(k).wait_send()
                to_outer(k).wait_send()
                own_out(k).wait()
                return 0

            lax.fori_loop(0, n_chunk, done, 0)

        def drain(h, _):
            x_fwd(h).wait_send()
            g_own(h).wait_send()
            g_other(h).wait_send()
            return 0

        lax.fori_loop(0, H, drain, 0)

        def drain_w(t, _):
            w_y(t).wait_send()
            pair(t).wait_send()
            return 0

        lax.fori_loop(0, 9, drain_w, 0)
        w_core.wait_send()
        for k in range(2):
            vecs_r[k].wait_send()
            dz_r[k].wait_send()
            z_l[k].wait()
            z_r[k].wait_send()
            z_w[k].wait_recv()


def solution(mesh):
    act_spec = P('stage', ('dp', 'tp'))
    w_spec = P('stage', None, None, None, 'tp')
    vec_spec = P('stage', 'tp')
    chan_spec = P('stage', 'dp', None, None, 'tp')

    def device_step(act_in, w_conv, gamma_vec, beta_vec, z_grad):
        on_conv = lax.axis_index('stage') == 1
        N, H, WD, CI = act_in.shape[1:]
        CO = w_conv.shape[-1]
        R = WD * N
        RP = 128 + 2 * PAD
        n_chunk = 18
        x = act_in[0].transpose(1, 2, 0, 3).reshape(H, R, CI)
        w = w_conv[0].reshape(9, CI, CO)
        dz = z_grad[0].transpose(1, 2, 0, 3).reshape(H, WD, 4, N, CO)
        any_spec = pl.BlockSpec(memory_space=pl.ANY)
        dma = pltpu.SemaphoreType.DMA
        z, dx, dw = pl.pallas_call(
            functools.partial(block_kernel, H, WD, CI, CO, n_chunk),
            out_shape=(
                jax.ShapeDtypeStruct((H, WD, 4, N, CO), BF16),
                jax.ShapeDtypeStruct((H, R, CI), BF16),
                jax.ShapeDtypeStruct((9, CI, CO), F32),
            ),
            in_specs=[any_spec] * 5,
            out_specs=(any_spec,) * 3,
            scratch_shapes=[
                pltpu.VMEM((2, H + 2, RP, CI), BF16),
                pltpu.VMEM((2, H + 2, RP - 16, CI), BF16),
                pltpu.VMEM((2, H + 2, RP, 2 * CO), BF16),
                pltpu.VMEM((2, H + 2, RP - 16, 2 * CO), BF16),
                pltpu.VMEM((4, 9, CI, CO), BF16),
                pltpu.VMEM((2, 2, H, WD, N, CO), BF16),
                pltpu.VMEM((2, 2, H, WD, N, CO), BF16),
                pltpu.VMEM((2, 2, 1, CO), F32),
                pltpu.VMEM((2, 9, CI, CO), F32),
                pltpu.VMEM((9, CI, CO), F32),
                pltpu.VMEM((n_chunk, CI // 2, CO), F32),
                pltpu.VMEM((n_chunk, CI // 2, CO), F32),
                pltpu.VMEM((n_chunk, CI // 2, CO), F32),
                pltpu.VMEM((CI, 256), BF16),
                pltpu.VMEM((H, R, 2 * CO), BF16),
                pltpu.VMEM((H, R, CI), BF16),
                dma((H,)), dma((2, H)), dma((H,)), dma((2, H)), dma((2, H)), dma((H,)), dma((H,)),
                dma, dma((3, 9)), dma((4, 9)), dma((2,)), dma((3,)), dma((3,)), dma((2,)), dma((2,)), dma((2,)),
                dma((2,)), dma((2,)), dma((2,)), dma((9,)), dma((9,)),
                dma((n_chunk,)), dma((n_chunk,)), dma((n_chunk,)), dma((n_chunk,)), dma((n_chunk,)), dma((n_chunk,)), dma((n_chunk,)), dma((H,)),
            ],
            compiler_params=pltpu.CompilerParams(collective_id=0, has_side_effects=True, vmem_limit_bytes=64 * 1024 * 1024 - 65536),
        )(x, w, gamma_vec, beta_vec, dz)
        z_full = z.reshape(H, WD, 4 * N, CO).transpose(2, 0, 1, 3)
        dx_full = dx.reshape(H, WD, N, CI).transpose(2, 0, 1, 3)
        dw_full = dw.reshape(3, 3, CI, CO)
        z_keep = jnp.where(on_conv, z_full, jnp.zeros_like(z_full))
        dx_keep = jnp.where(on_conv, jnp.zeros_like(dx_full), dx_full)
        w_keep = jnp.where(on_conv, dw_full, jnp.zeros_like(dw_full))
        return z_keep[None], dx_keep[None], w_keep[None]

    return jax.shard_map(device_step, mesh=mesh, in_specs=(act_spec, w_spec, vec_spec, vec_spec, chan_spec), out_specs=(chan_spec, act_spec, w_spec), check_vma=False)
```

time: 334 us -> 161 us (0.48)
  waiting for transfers between devices: 252 us -> 0 us
  Pallas kernels: 0 us -> 152 us
  matrix products: 49.8 us -> 0 us
  between operations: 13.8 us -> 0.65 us
  starting transfers between devices: 5.34 us -> 0 us
    pallas_call x0 -> x1, Pallas kernels: none -> 152 us  [device_step(): pl.pallas_call(functools.partial(block_kernel, H, WD, CI, CO, n_chunk), o...]
    psum x1 -> x0, waiting for transfers between devices: 87.8 us -> none  [device_step(): w_total = lax.psum(w_part, 'dp')]
    reduce_scatter x1 -> x0, waiting for transfers between devices: 78.6 us -> none  [device_step(): lax.psum_scatter(act_part, 'tp', scatter_dimension=0, tiled=True)]
    conv_general_dilated x3 -> x0, matrix products: 49.8 us -> none  [the longest x1 19.2 us: conv_fwd(): lax.conv_general_dilated(images, kernel, (1, 1), 'SAME', dimension_number...]
    all_gather x1 -> x0, waiting for transfers between devices: 48.5 us -> none  [device_step(): group_act = lax.all_gather(arrived, 'tp', axis=0, tiled=True)]
    ppermute x2 -> x0, waiting for transfers between devices: 37.4 us -> none  [the longest x1 37.4 us: device_step(): arrived = lax.ppermute(act_in[0], 'stage', perm=[(0, 1)])]
    ppermute x2 -> x0, starting transfers between devices: 5.04 us -> none  [the longest x1 3.62 us: device_step(): act_back = lax.ppermute(act_mine, 'stage', perm=[(1, 0)])]
  transfers between devices with their start and end apart: 5 -> 0, of which waited for: 4 -> 0; matrix products, arithmetic and copies ran while one was open for 8% -> 0% of each run, Pallas kernels for 0% -> 0%
where the time goes in v1:
time: 161 us; the launch traced here: 159 us
  Pallas kernels  152 us (94%)
  other arithmetic  5.67 us (4%)
    pallas_call x1, Pallas kernels, device_step(): pl.pallas_call(functools.partial(block_kernel, H, WD, CI, CO, n_chunk), o...  152 us
    broadcast_in_dim x2, other arithmetic, device_step(): return (z_keep[None], dx_keep[None], w_keep[None])  4.07 us

profile of v1, /device:TPU:4, one launch (start us, length us, event | category | flops | bytes accessed | tf_op | source)
XLA Modules:
  0.0 159.2 jit_solution(10499814963911098426)
XLA Ops:
  0.6 151.9 %shard_map.76 = (bf16[14,14,4,8,128]{4,3,2,1,0:T(8,128)(2,1)}, bf16[14,112,512]{2,1,0:T(8,128)(2,1)}, f32[9,512,128]{2,1,0:T(8,128)}) custom-call(bf16[14,112,512]{2,1,0:T(8,128)(2,1)} %bitcast.25, bf16[9,512,128]{2,1,0:T(8,128)(2,1)} %bitcast.27, f32[1,128]{1,0:T(1,128)} %gam_ref.1, f32[1,128]{1,0:T(1,128)} %bet_ref.1, bf16[14,14,4,8,128]{4,3,2,1,0:T(8,128)(2,1)} %bitcast.26), custom_call_target="tpu_custom_call" | custom-call | tf_op jit(solution)/shard_map/pallas_call | solution.py:415
  152.6 0.0 copy-start.1
  152.6 2.8 %select_bitcast_fusion.1 = bf16[1,32,14,14,128]{4,1,3,2,0:T(8,128)(2,1)} fusion(bf16[14,14,4,8,128]{4,3,2,1,0:T(8,128)(2,1)} %get-tuple-element.6, pred[]{:T(512)S(6)} %eq.3), kind=kLoop, calls=%fused_computation.1 | loop fusion | flops 802816 | bytes 3211265 | tf_op jit(solution)/shard_map/broadcast_in_dim | solution.py:454
  155.4 0.0 copy-done.1
  155.4 0.0 copy-start
  155.4 1.3 select_bitcast_fusion
  156.7 1.0 copy-done
  157.6 1.6 %broadcast_select_fusion = f32[9,512,128]{2,1,0:T(8,128)} fusion(f32[9,512,128]{2,1,0:T(8,128)S(1)} %copy-done, pred[]{:T(512)S(6)} %eq.3), kind=kLoop, calls=%fused_computation.2 | loop fusion | flops 589824 | bytes 4718593 | tf_op jit(solution)/shard_map/jit(_where)/select_n | solution.py:453
Async XLA Ops:
  152.6 2.8 %copy-start.1 = (bf16[14,112,512]{2,1,0:T(8,128)(2,1)S(1)}, bf16[14,112,512]{2,1,0:T(8,128)(2,1)}, u32[]{:S(2)}) copy-start(bf16[14,112,512]{2,1,0:T(8,128)(2,1)} %get-tuple-element.7) | copy-start | bytes 4816900
  155.4 2.2 %copy-start = (f32[9,512,128]{2,1,0:T(8,128)S(1)}, f32[9,512,128]{2,1,0:T(8,128)}, u32[]{:S(2)}) copy-start(f32[9,512,128]{2,1,0:T(8,128)} %get-tuple-element.8) | copy-start | bytes 7077892

commit v2 on v1

--- a/solution.py
+++ b/solution.py
@@ -11,6 +11,7 @@
 F32 = jnp.float32
 BF16 = jnp.bfloat16
 PAD = 16
+AHEAD = 2
 
 
 def remote(src, dst, send_sem, recv_sem, dev):
@@ -132,11 +133,19 @@
         def dx_out(h):
             return pltpu.make_async_copy(dxb.at[h], dx_ref.at[h], s_dx.at[h])
 
+        def g_relay(j):
+            relay_in(j).wait_recv()
+            relay_out(j).start()
+
+        lax.fori_loop(0, AHEAD, lambda j, _: (g_relay(j), 0)[1], 0)
+
         def g_step(j, _):
+            @pl.when(j + AHEAD < H)
+            def _():
+                g_relay(j + AHEAD)
+
             @pl.when(j < H)
             def _():
-                relay_in(j).wait_recv()
-                relay_out(j).start()
                 g_in(j, xi).wait_recv()
                 g_in(j, 1 - xi).wait_recv()
                 for b in range(2):
@@ -230,11 +239,19 @@
         def g_other(h):
             return remote(ge.at[1 - xi, h + 1, pl.ds(PAD, R), :], relay.at[h], s_gs.at[1, h], s_gl.at[h], y_dev)
 
+        def x_relay(j):
+            x_in(j, xi).wait_recv()
+            x_fwd(j).start()
+
+        lax.fori_loop(0, AHEAD, lambda j, _: (x_relay(j), 0)[1], 0)
+
         def step(j, _):
+            @pl.when(j + AHEAD < H)
+            def _():
+                x_relay(j + AHEAD)
+
             @pl.when(j < H)
             def _():
-                x_in(j, xi).wait_recv()
-                x_fwd(j).start()
                 x_in(j, 1 - xi).wait_recv()
                 for s in range(2):
                     odd_copy(xe, xo, s, j + 1)

time: 161 us -> 122 us (0.76)
  Pallas kernels: 152 us -> 114 us
    pallas_call x1, Pallas kernels: 152 us -> 114 us  [device_step(): pl.pallas_call(functools.partial(block_kernel, H, WD, CI, CO, n_chunk), o...]
where the time goes in v2:
time: 122 us; the launch traced here: 121 us
  Pallas kernels  114 us (93%)
  other arithmetic  5.67 us (5%)
    pallas_call x1, Pallas kernels, device_step(): pl.pallas_call(functools.partial(block_kernel, H, WD, CI, CO, n_chunk), o...  114 us
    broadcast_in_dim x2, other arithmetic, device_step(): return (z_keep[None], dx_keep[None], w_keep[None])  4.07 us

profile of v2, /device:TPU:4, one launch (start us, length us, event | category | flops | bytes accessed | tf_op | source)
XLA Modules:
  0.0 121.5 jit_solution(2835377112884278133)
XLA Ops:
  0.6 114.2 %shard_map.76 = (bf16[14,14,4,8,128]{4,3,2,1,0:T(8,128)(2,1)}, bf16[14,112,512]{2,1,0:T(8,128)(2,1)}, f32[9,512,128]{2,1,0:T(8,128)}) custom-call(bf16[14,112,512]{2,1,0:T(8,128)(2,1)} %bitcast.25, bf16[9,512,128]{2,1,0:T(8,128)(2,1)} %bitcast.27, f32[1,128]{1,0:T(1,128)} %gam_ref.1, f32[1,128]{1,0:T(1,128)} %bet_ref.1, bf16[14,14,4,8,128]{4,3,2,1,0:T(8,128)(2,1)} %bitcast.26), custom_call_target="tpu_custom_call" | custom-call | tf_op jit(solution)/shard_map/pallas_call | solution.py:432
  114.8 0.0 copy-start.1
  114.8 2.8 %select_bitcast_fusion.1 = bf16[1,32,14,14,128]{4,1,3,2,0:T(8,128)(2,1)} fusion(bf16[14,14,4,8,128]{4,3,2,1,0:T(8,128)(2,1)} %get-tuple-element.6, pred[]{:T(512)S(6)} %eq.3), kind=kLoop, calls=%fused_computation.1 | loop fusion | flops 802816 | bytes 3211265 | tf_op jit(solution)/shard_map/broadcast_in_dim | solution.py:471
  117.6 0.0 copy-done.1
  117.6 0.0 copy-start
  117.6 1.3 %select_bitcast_fusion = bf16[1,8,14,14,512]{4,1,3,2,0:T(8,128)(2,1)} fusion(bf16[14,112,512]{2,1,0:T(8,128)(2,1)S(1)} %copy-done.1, pred[]{:T(512)S(6)} %eq.3), kind=kLoop, calls=%fused_computation | loop fusion | flops 802816 | bytes 3211265 | tf_op jit(solution)/shard_map/broadcast_in_dim | solution.py:471
  118.9 1.0 copy-done
  119.9 1.6 %broadcast_select_fusion = f32[9,512,128]{2,1,0:T(8,128)} fusion(f32[9,512,128]{2,1,0:T(8,128)S(1)} %copy-done, pred[]{:T(512)S(6)} %eq.3), kind=kLoop, calls=%fused_computation.2 | loop fusion | flops 589824 | bytes 4718593 | tf_op jit(solution)/shard_map/jit(_where)/select_n | solution.py:470
Async XLA Ops:
  114.8 2.8 %copy-start.1 = (bf16[14,112,512]{2,1,0:T(8,128)(2,1)S(1)}, bf16[14,112,512]{2,1,0:T(8,128)(2,1)}, u32[]{:S(2)}) copy-start(bf16[14,112,512]{2,1,0:T(8,128)(2,1)} %get-tuple-element.7) | copy-start | bytes 4816900
  117.6 2.2 %copy-start = (f32[9,512,128]{2,1,0:T(8,128)S(1)}, f32[9,512,128]{2,1,0:T(8,128)}, u32[]{:S(2)}) copy-start(f32[9,512,128]{2,1,0:T(8,128)} %get-tuple-element.8) | copy-start | bytes 7077892

commit v3 on v2

--- a/solution.py
+++ b/solution.py
@@ -19,9 +19,9 @@
 
 
 def block_kernel(H, WD, CI, CO, n_chunk, x_ref, w_ref, gam_ref, bet_ref, dz_ref, z_ref, dx_ref, dw_ref,
-                 xe, xo, ge, go, wall, dzb, zb, vec, acc, prx, pb, rb, mb, xt, relay, dxb, *sems):
+                 xe, xo, ge, go, wall, dzb, zb, vec, acc, prx, pb, rb, mb, xt, relay, *sems):
     (s_xs, s_xr, s_xf, s_gs, s_gr, s_gl, s_gf, s_wl, s_ws, s_wr, s_vl, s_vs, s_vr, s_dl, s_ds, s_dr,
-     s_zl, s_zs, s_zr, s_ps, s_pr, s_os, s_or, s_ms, s_mr, s_ts, s_tr, s_tl, s_dx) = sems
+     s_zs, s_zr, s_ps, s_pr, s_os, s_or, s_ms, s_mr, s_ts, s_tr) = sems
     R = WD * 8
     CW = 2 * CO
     zi = lax.axis_index("dp")
@@ -91,6 +91,18 @@
         zero_planes(ge)
         zero_planes(go)
 
+        def zero_out(h, _):
+            z_ref[h] = jnp.zeros(z_ref.shape[1:], BF16)
+            return 0
+
+        lax.fori_loop(0, H, zero_out, 0)
+
+        def zero_dw(t, _):
+            dw_ref[t] = jnp.zeros((CI, CO), F32)
+            return 0
+
+        lax.fori_loop(0, 9, zero_dw, 0)
+
         def w_in(t, b):
             return remote(wall.at[b, t], wall.at[b, t], s_ws.at[0, t], s_wr.at[b, t], y_dev)
 
@@ -129,9 +141,6 @@
 
         def relay_out(j):
             return remote(relay.at[j], ge.at[xi, j + 1, pl.ds(PAD, R), :], s_gf.at[j], s_gr.at[xi, j], x_dev)
-
-        def dx_out(h):
-            return pltpu.make_async_copy(dxb.at[h], dx_ref.at[h], s_dx.at[h])
 
         def g_relay(j):
             relay_in(j).wait_recv()
@@ -162,8 +171,7 @@
                             lhs = tap_rows(ge, go, b, h + 2 - ky, 1 - kx, R)
                             rhs = jnp.concatenate([wall[2 * b, t], wall[2 * b + 1, t]], axis=1)
                             tot = tot + lax.dot_general(lhs, rhs, (((1,), (1,)), ((), ())), preferred_element_type=F32)
-                dxb[h] = tot.astype(BF16)
-                dx_out(h).start()
+                dx_ref[h] = tot.astype(BF16)
 
             return 0
 
@@ -172,7 +180,6 @@
         def drain(h, _):
             x_copy(h).wait_send()
             relay_out(h).wait_send()
-            dx_out(h).wait()
             return 0
 
         lax.fori_loop(0, H, drain, 0)
@@ -217,6 +224,12 @@
             return 0
 
         lax.fori_loop(0, 9, zero_acc, 0)
+
+        def zero_dx(h, _):
+            dx_ref[h] = jnp.zeros((R, CI), BF16)
+            return 0
+
+        lax.fori_loop(0, H, zero_dx, 0)
         for k in range(2):
             vecs_l[k].wait()
             vecs_r[k].wait_recv()
@@ -278,6 +291,7 @@
                 g_other(h).start()
                 for s in range(2):
                     odd_copy(ge, go, s, h + 1)
+                    z_ref[h, :, 2 * s + c] = zb[s, c, h]
 
             @pl.when(j >= 2)
             def _():
@@ -300,11 +314,9 @@
             return remote(acc.at[1 - c, t], prx.at[t], s_ps.at[t], s_pr.at[t], c_dev)
 
         lax.fori_loop(0, 9, lambda t, _: (pair(t).start(), 0)[1], 0)
-        z_l = [pltpu.make_async_copy(zb.at[s, c], z_ref.at[:, :, 2 * s + c], s_zl.at[s]) for s in range(2)]
         z_r = [remote(zb.at[s, 1 - c], z_ref.at[:, :, 2 * s + c], s_zs.at[s], s_zr.at[s], c_dev) for s in range(2)]
         z_w = [remote(zb.at[s, 1 - c], z_ref.at[:, :, 2 * s + 1 - c], s_zs.at[s], s_zr.at[s], c_dev) for s in range(2)]
         for s in range(2):
-            z_l[s].start()
             z_r[s].start()
 
         half = CI // 2
@@ -332,13 +344,10 @@
             return remote(pb.at[k], mb.at[k], s_ms.at[k], s_mr.at[k], mate_dev)
 
         def to_outer(k):
-            return remote(rb.at[k], dw_view(k), s_ts.at[k], s_tr.at[k], outer_dev)
+            return remote(dw_view(k), dw_view(k), s_ts.at[k], s_tr.at[k], outer_dev)
 
         def from_inner(k):
-            return remote(rb.at[k], dw_view(k), s_ts.at[k], s_tr.at[k], inner_dev)
-
-        def own_out(k):
-            return pltpu.make_async_copy(rb.at[k], dw_view(k), s_tl.at[k])
+            return remote(dw_view(k), dw_view(k), s_ts.at[k], s_tr.at[k], inner_dev)
 
         @pl.when(jnp.logical_not(inner))
         def _():
@@ -372,9 +381,8 @@
                 def _():
                     m = k - LAG
                     to_mate(m).wait_recv()
-                    rb[m] = pb[m] + mb[m]
+                    dw_ref[m // 2, pl.ds(pl.multiple_of((m % 2) * half, half), half), :] = pb[m] + mb[m]
                     to_outer(m).start()
-                    own_out(m).start()
 
                 return 0
 
@@ -383,7 +391,6 @@
             def done(k, _):
                 to_mate(k).wait_send()
                 to_outer(k).wait_send()
-                own_out(k).wait()
                 return 0
 
             lax.fori_loop(0, n_chunk, done, 0)
@@ -406,9 +413,28 @@
         for k in range(2):
             vecs_r[k].wait_send()
             dz_r[k].wait_send()
-            z_l[k].wait()
             z_r[k].wait_send()
             z_w[k].wait_recv()
+
+
+def out_kernel(*refs):
+    srcs, dsts, sem = refs[:3], refs[3:6], refs[6]
+    copies = [pltpu.make_async_copy(a, b, sem.at[i]) for i, (a, b) in enumerate(zip(srcs, dsts))]
+    for cp in copies:
+        cp.start()
+    for cp in copies:
+        cp.wait()
+
+
+def write_out(*arrays):
+    return pl.pallas_call(
+        out_kernel,
+        out_shape=tuple(jax.ShapeDtypeStruct(a.shape, a.dtype) for a in arrays),
+        in_specs=[pl.BlockSpec(memory_space=pltpu.VMEM)] * 3,
+        out_specs=(pl.BlockSpec(memory_space=pl.ANY),) * 3,
+        scratch_shapes=[pltpu.SemaphoreType.DMA((3,))],
+        compiler_params=pltpu.CompilerParams(vmem_limit_bytes=16 * 1024 * 1024),
+    )(*arrays)
 
 
 def solution(mesh):
@@ -418,7 +444,6 @@
     chan_spec = P('stage', 'dp', None, None, 'tp')
 
     def device_step(act_in, w_conv, gamma_vec, beta_vec, z_grad):
-        on_conv = lax.axis_index('stage') == 1
         N, H, WD, CI = act_in.shape[1:]
         CO = w_conv.shape[-1]
         R = WD * N
@@ -427,7 +452,6 @@
         x = act_in[0].transpose(1, 2, 0, 3).reshape(H, R, CI)
         w = w_conv[0].reshape(9, CI, CO)
         dz = z_grad[0].transpose(1, 2, 0, 3).reshape(H, WD, 4, N, CO)
-        any_spec = pl.BlockSpec(memory_space=pl.ANY)
         dma = pltpu.SemaphoreType.DMA
         z, dx, dw = pl.pallas_call(
             functools.partial(block_kernel, H, WD, CI, CO, n_chunk),
@@ -436,8 +460,8 @@
                 jax.ShapeDtypeStruct((H, R, CI), BF16),
                 jax.ShapeDtypeStruct((9, CI, CO), F32),
             ),
-            in_specs=[any_spec] * 5,
-            out_specs=(any_spec,) * 3,
+            in_specs=[pl.BlockSpec(memory_space=pltpu.HBM)] * 5,
+            out_specs=(pl.BlockSpec(memory_space=pltpu.VMEM),) * 3,
             scratch_shapes=[
                 pltpu.VMEM((2, H + 2, RP, CI), BF16),
                 pltpu.VMEM((2, H + 2, RP - 16, CI), BF16),
@@ -454,20 +478,17 @@
                 pltpu.VMEM((n_chunk, CI // 2, CO), F32),
                 pltpu.VMEM((CI, 256), BF16),
                 pltpu.VMEM((H, R, 2 * CO), BF16),
-                pltpu.VMEM((H, R, CI), BF16),
                 dma((H,)), dma((2, H)), dma((H,)), dma((2, H)), dma((2, H)), dma((H,)), dma((H,)),
                 dma, dma((3, 9)), dma((4, 9)), dma((2,)), dma((3,)), dma((3,)), dma((2,)), dma((2,)), dma((2,)),
-                dma((2,)), dma((2,)), dma((2,)), dma((9,)), dma((9,)),
-                dma((n_chunk,)), dma((n_chunk,)), dma((n_chunk,)), dma((n_chunk,)), dma((n_chunk,)), dma((n_chunk,)), dma((n_chunk,)), dma((H,)),
+                dma((2,)), dma((2,)), dma((9,)), dma((9,)),
+                dma((n_chunk,)), dma((n_chunk,)), dma((n_chunk,)), dma((n_chunk,)), dma((n_chunk,)), dma((n_chunk,)),
             ],
-            compiler_params=pltpu.CompilerParams(collective_id=0, has_side_effects=True, vmem_limit_bytes=64 * 1024 * 1024 - 65536),
-        )(x, w, gamma_vec, beta_vec, dz)
+            compiler_params=pltpu.CompilerParams(collective_id=0, has_side_effects=True, vmem_limit_bytes=46 * 1024 * 1024),
+        )(*[pltpu.with_memory_space_constraint(a, pltpu.HBM) for a in (x, w, gamma_vec, beta_vec, dz)])
+        z, dx, dw = write_out(z, dx, dw)
         z_full = z.reshape(H, WD, 4 * N, CO).transpose(2, 0, 1, 3)
         dx_full = dx.reshape(H, WD, N, CI).transpose(2, 0, 1, 3)
         dw_full = dw.reshape(3, 3, CI, CO)
-        z_keep = jnp.where(on_conv, z_full, jnp.zeros_like(z_full))
-        dx_keep = jnp.where(on_conv, jnp.zeros_like(dx_full), dx_full)
-        w_keep = jnp.where(on_conv, dw_full, jnp.zeros_like(dw_full))
-        return z_keep[None], dx_keep[None], w_keep[None]
+        return z_full[None], dx_full[None], dw_full[None]
 
     return jax.shard_map(device_step, mesh=mesh, in_specs=(act_spec, w_spec, vec_spec, vec_spec, chan_spec), out_specs=(chan_spec, act_spec, w_spec), check_vma=False)

time: 122 us -> 117 us (0.959)
  other arithmetic: 5.67 us -> 0 us
  Pallas kernels: 114 us -> 116 us
    broadcast_in_dim x2 -> x0, other arithmetic: 4.07 us -> none  [device_step(): return (z_keep[None], dx_keep[None], w_keep[None])]
    pallas_call x0 -> x1, Pallas kernels: none -> 2.49 us  [write_out(): pl.pallas_call(out_kernel, out_shape=tuple((jax.ShapeDtypeStruct(a.shape,...]
    select_n x1 -> x0, other arithmetic: 1.6 us -> none  [device_step(): w_keep = jnp.where(on_conv, dw_full, jnp.zeros_like(dw_full))]
where the time goes in v3:
time: 117 us
  Pallas kernels  116 us (99%)
    pallas_call x1, Pallas kernels, device_step(): pl.pallas_call(functools.partial(block_kernel, H, WD, CI, CO, n_chunk), o...  114 us
    pallas_call x1, Pallas kernels, write_out(): pl.pallas_call(out_kernel, out_shape=tuple((jax.ShapeDtypeStruct(a.shape,...  2.49 us

profile of v3, /device:TPU:4, one launch (start us, length us, event | category | flops | bytes accessed | tf_op | source)
XLA Modules:
  0.0 117.0 jit_solution(17614038489848877292)
XLA Ops:
  0.6 113.9 %shard_map.76 = (bf16[14,14,4,8,128]{4,3,2,1,0:T(8,128)(2,1)S(1)}, bf16[14,112,512]{2,1,0:T(8,128)(2,1)S(1)}, f32[9,512,128]{2,1,0:T(8,128)S(1)}) custom-call(bf16[14,112,512]{2,1,0:T(8,128)(2,1)} %bitcast.22, bf16[9,512,128]{2,1,0:T(8,128)(2,1)} %bitcast.24, f32[1,128]{1,0:T(1,128)} %gam_ref.1, f32[1,128]{1,0:T(1,128)} %bet_ref.1, ...), custom_call_target="tpu_custom_call" | custom-call | tf_op jit(solution)/shard_map/pallas_call | solution.py:456
  114.5 2.5 %shard_map.77 = (bf16[14,14,4,8,128]{4,3,2,1,0:T(8,128)(2,1)}, bf16[14,112,512]{2,1,0:T(8,128)(2,1)}, f32[9,512,128]{2,1,0:T(8,128)}) custom-call(bf16[14,14,4,8,128]{4,3,2,1,0:T(8,128)(2,1)S(1)} %get-tuple-element.9.refs_0_, bf16[14,112,512]{2,1,0:T(8,128)(2,1)S(1)} %get-tuple-element.10.refs_1_, f32[9,512,128]{2,1,0:T(8,128)S(1)} %get-tuple-element.11.refs_2_), custom_call_target="tpu_custom_call" | custom-call | tf_op jit(solution)/shard_map/pallas_call | solution.py:430

commit v4 on v3

--- a/solution.py
+++ b/solution.py
@@ -12,6 +12,8 @@
 BF16 = jnp.bfloat16
 PAD = 16
 AHEAD = 2
+LAG = 2
+N_B = 5
 
 
 def remote(src, dst, send_sem, recv_sem, dev):
@@ -21,8 +23,11 @@
 def block_kernel(H, WD, CI, CO, n_chunk, x_ref, w_ref, gam_ref, bet_ref, dz_ref, z_ref, dx_ref, dw_ref,
                  xe, xo, ge, go, wall, dzb, zb, vec, acc, prx, pb, rb, mb, xt, relay, *sems):
     (s_xs, s_xr, s_xf, s_gs, s_gr, s_gl, s_gf, s_wl, s_ws, s_wr, s_vl, s_vs, s_vr, s_dl, s_ds, s_dr,
-     s_zs, s_zr, s_ps, s_pr, s_os, s_or, s_ms, s_mr, s_ts, s_tr) = sems
+     s_zs, s_zr, s_ps, s_pr, s_os, s_or, s_ms, s_mr, s_ts, s_tr,
+     s_bs, s_br, s_us, s_ur) = sems
     R = WD * 8
+    half = CI // 2
+    n_a = n_chunk - N_B
     CW = 2 * CO
     zi = lax.axis_index("dp")
     st = lax.axis_index("stage")
@@ -81,6 +86,18 @@
         start = PAD + 8 * shift - 8
         return odd[s, plane, start:start + n, :]
 
+    def dw_view(k):
+        return dw_ref.at[k // 2, pl.ds(pl.multiple_of((k % 2) * half, half), half), :]
+
+    def part_up(k):
+        return remote(pb.at[k], pb.at[k], s_os.at[k], s_or.at[k], y_dev)
+
+    def to_mate(k):
+        return remote(pb.at[k], mb.at[k], s_ms.at[k], s_mr.at[k], mate_dev)
+
+    def total_down(src, k):
+        return remote(src.at[k], dw_view(k), s_ts.at[k], s_tr.at[k], y_dev)
+
     @pl.when(st == 0)
     def _():
         def x_copy(h):
@@ -176,6 +193,65 @@
             return 0
 
         lax.fori_loop(0, H + 1, g_step, 0)
+
+        def b_to_inner(k, dev):
+            return remote(pb.at[k], rb.at[k], s_bs.at[k], s_br.at[k], dev)
+
+        def b_to_outer(k, dev):
+            return remote(rb.at[k], mb.at[k], s_us.at[k], s_ur.at[k], dev)
+
+        @pl.when(jnp.logical_not(inner))
+        def _():
+            def up(k, _):
+                part_up(k).wait_recv()
+                b_to_inner(k, inner_dev).start()
+                return 0
+
+            lax.fori_loop(n_a, n_chunk, up, 0)
+
+            def down(k, _):
+                b_to_outer(k, inner_dev).wait_recv()
+                total_down(mb, k).start()
+                return 0
+
+            lax.fori_loop(n_a, n_chunk, down, 0)
+
+            def done(k, _):
+                b_to_inner(k, inner_dev).wait_send()
+                total_down(mb, k).wait_send()
+                return 0
+
+            lax.fori_loop(n_a, n_chunk, done, 0)
+
+        @pl.when(inner)
+        def _():
+            def both(k, _):
+                @pl.when(k < n_chunk)
+                def _():
+                    part_up(k).wait_recv()
+                    b_to_inner(k, outer_dev).wait_recv()
+                    pb[k] = pb[k] + rb[k]
+                    to_mate(k).start()
+
+                @pl.when(k >= n_a + LAG)
+                def _():
+                    m = k - LAG
+                    to_mate(m).wait_recv()
+                    rb[m] = pb[m] + mb[m]
+                    b_to_outer(m, outer_dev).start()
+                    total_down(rb, m).start()
+
+                return 0
+
+            lax.fori_loop(n_a, n_chunk + LAG, both, 0)
+
+            def done(k, _):
+                to_mate(k).wait_send()
+                b_to_outer(k, outer_dev).wait_send()
+                total_down(rb, k).wait_send()
+                return 0
+
+            lax.fori_loop(n_a, n_chunk, done, 0)
 
         def drain(h, _):
             x_copy(h).wait_send()
@@ -313,35 +389,37 @@
         def pair(t):
             return remote(acc.at[1 - c, t], prx.at[t], s_ps.at[t], s_pr.at[t], c_dev)
 
-        lax.fori_loop(0, 9, lambda t, _: (pair(t).start(), 0)[1], 0)
+        lax.fori_loop(0, 9, lambda i, _: (pair((i + n_a // 2) % 9).start(), 0)[1], 0)
         z_r = [remote(zb.at[s, 1 - c], z_ref.at[:, :, 2 * s + c], s_zs.at[s], s_zr.at[s], c_dev) for s in range(2)]
         z_w = [remote(zb.at[s, 1 - c], z_ref.at[:, :, 2 * s + 1 - c], s_zs.at[s], s_zr.at[s], c_dev) for s in range(2)]
         for s in range(2):
             z_r[s].start()
 
-        half = CI // 2
-
-        def own_part(k):
+        def own_part(k, fresh):
             t = k // 2
             q = pl.multiple_of((k % 2) * half, half)
 
-            @pl.when(k % 2 == 0)
+            @pl.when(fresh)
             def _():
                 pair(t).wait_recv()
 
             return acc[c, t, pl.ds(q, half), :] + prx[t, pl.ds(q, half), :]
 
-        def dw_view(k):
-            return dw_ref.at[k // 2, pl.ds(pl.multiple_of((k % 2) * half, half), half), :]
+        def part_a(k):
+            return own_part(k, jnp.logical_and(k % 2 == 0, k // 2 < n_a // 2))
+
+        def send_b(k, _):
+            pb[k] = own_part(k, jnp.logical_or(k % 2 == 0, k == n_a))
+            part_up(k).start()
+            return 0
+
+        lax.fori_loop(n_a, n_chunk, send_b, 0)
 
         def to_inner(k):
             return remote(pb.at[k], rb.at[k], s_os.at[k], s_or.at[k], inner_dev)
 
         def from_outer(k):
             return remote(pb.at[k], rb.at[k], s_os.at[k], s_or.at[k], outer_dev)
-
-        def to_mate(k):
-            return remote(pb.at[k], mb.at[k], s_ms.at[k], s_mr.at[k], mate_dev)
 
         def to_outer(k):
             return remote(dw_view(k), dw_view(k), s_ts.at[k], s_tr.at[k], outer_dev)
@@ -352,27 +430,25 @@
         @pl.when(jnp.logical_not(inner))
         def _():
             def send(k, _):
-                pb[k] = own_part(k)
+                pb[k] = part_a(k)
                 to_inner(k).start()
                 return 0
 
-            lax.fori_loop(0, n_chunk, send, 0)
+            lax.fori_loop(0, n_a, send, 0)
 
             def take(k, _):
                 from_inner(k).wait_recv()
                 to_inner(k).wait_send()
                 return 0
 
-            lax.fori_loop(0, n_chunk, take, 0)
+            lax.fori_loop(0, n_a, take, 0)
 
         @pl.when(inner)
         def _():
-            LAG = 2
-
             def both(k, _):
-                @pl.when(k < n_chunk)
+                @pl.when(k < n_a)
                 def _():
-                    part = own_part(k)
+                    part = part_a(k)
                     from_outer(k).wait_recv()
                     pb[k] = part + rb[k]
                     to_mate(k).start()
@@ -386,14 +462,21 @@
 
                 return 0
 
-            lax.fori_loop(0, n_chunk + LAG, both, 0)
+            lax.fori_loop(0, n_a + LAG, both, 0)
 
             def done(k, _):
                 to_mate(k).wait_send()
                 to_outer(k).wait_send()
                 return 0
 
-            lax.fori_loop(0, n_chunk, done, 0)
+            lax.fori_loop(0, n_a, done, 0)
+
+        def done_b(k, _):
+            total_down(rb, k).wait_recv()
+            part_up(k).wait_send()
+            return 0
+
+        lax.fori_loop(n_a, n_chunk, done_b, 0)
 
         def drain(h, _):
             x_fwd(h).wait_send()
@@ -481,7 +564,7 @@
                 dma((H,)), dma((2, H)), dma((H,)), dma((2, H)), dma((2, H)), dma((H,)), dma((H,)),
                 dma, dma((3, 9)), dma((4, 9)), dma((2,)), dma((3,)), dma((3,)), dma((2,)), dma((2,)), dma((2,)),
                 dma((2,)), dma((2,)), dma((9,)), dma((9,)),
-                dma((n_chunk,)), dma((n_chunk,)), dma((n_chunk,)), dma((n_chunk,)), dma((n_chunk,)), dma((n_chunk,)),
+                *[dma((n_chunk,))] * 10,
             ],
             compiler_params=pltpu.CompilerParams(collective_id=0, has_side_effects=True, vmem_limit_bytes=46 * 1024 * 1024),
         )(*[pltpu.with_memory_space_constraint(a, pltpu.HBM) for a in (x, w, gamma_vec, beta_vec, dz)])

time: 117 us -> 107 us (0.915); the launches traced: 117 us -> 106 us
  Pallas kernels: 116 us -> 105 us
    pallas_call x1, Pallas kernels: 114 us -> 102 us  [device_step(): pl.pallas_call(functools.partial(block_kernel, H, WD, CI, CO, n_chunk), o...]
where the time goes in v4:
time: 107 us; the launch traced here: 106 us
  Pallas kernels  105 us (98%)
    pallas_call x1, Pallas kernels, device_step(): pl.pallas_call(functools.partial(block_kernel, H, WD, CI, CO, n_chunk), o...  102 us
    pallas_call x1, Pallas kernels, write_out(): pl.pallas_call(out_kernel, out_shape=tuple((jax.ShapeDtypeStruct(a.shape,...  2.49 us

profile of v4, /device:TPU:4, one launch (start us, length us, event | category | flops | bytes accessed | tf_op | source)
XLA Modules:
  0.0 105.6 jit_solution(15239663987732410866)
XLA Ops:
  0.6 102.5 %shard_map.76 = (bf16[14,14,4,8,128]{4,3,2,1,0:T(8,128)(2,1)S(1)}, bf16[14,112,512]{2,1,0:T(8,128)(2,1)S(1)}, f32[9,512,128]{2,1,0:T(8,128)S(1)}) custom-call(bf16[14,112,512]{2,1,0:T(8,128)(2,1)} %bitcast.22, bf16[9,512,128]{2,1,0:T(8,128)(2,1)} %bitcast.24, f32[1,128]{1,0:T(1,128)} %gam_ref.1, f32[1,128]{1,0:T(1,128)} %bet_ref.1, ...), custom_call_target="tpu_custom_call" | custom-call | tf_op jit(solution)/shard_map/pallas_call | solution.py:539
  103.1 2.5 %shard_map.77 = (bf16[14,14,4,8,128]{4,3,2,1,0:T(8,128)(2,1)}, bf16[14,112,512]{2,1,0:T(8,128)(2,1)}, f32[9,512,128]{2,1,0:T(8,128)}) custom-call(bf16[14,14,4,8,128]{4,3,2,1,0:T(8,128)(2,1)S(1)} %get-tuple-element.9.refs_0_, bf16[14,112,512]{2,1,0:T(8,128)(2,1)S(1)} %get-tuple-element.10.refs_1_, f32[9,512,128]{2,1,0:T(8,128)S(1)} %get-tuple-element.11.refs_2_), custom_call_target="tpu_custom_call" | custom-call | tf_op jit(solution)/shard_map/pallas_call | solution.py:513

commit v5 on v4

--- a/solution.py
+++ b/solution.py
@@ -13,7 +13,7 @@
 PAD = 16
 AHEAD = 2
 LAG = 2
-N_B = 5
+N_B = 8
 
 
 def remote(src, dst, send_sem, recv_sem, dev):
@@ -27,6 +27,7 @@
      s_bs, s_br, s_us, s_ur) = sems
     R = WD * 8
     half = CI // 2
+    quarter = CI // 4
     n_a = n_chunk - N_B
     CW = 2 * CO
     zi = lax.axis_index("dp")
@@ -120,36 +121,6 @@
 
         lax.fori_loop(0, 9, zero_dw, 0)
 
-        def w_in(t, b):
-            return remote(wall.at[b, t], wall.at[b, t], s_ws.at[0, t], s_wr.at[b, t], y_dev)
-
-        def w_fwd(t, b, k, dev):
-            return remote(wall.at[b, t], wall.at[b, t], s_ws.at[k, t], s_wr.at[b, t], dev)
-
-        b_x = 2 * (1 - xi) + c
-
-        def w_step(t, _):
-            w_in(t, tp).wait_recv()
-            w_fwd(t, tp, 0, c_dev).start()
-            w_fwd(t, tp, 1, x_dev).start()
-            return 0
-
-        lax.fori_loop(0, 9, w_step, 0)
-
-        def w_step2(t, _):
-            w_in(t, b_x).wait_recv()
-            w_fwd(t, b_x, 2, c_dev).start()
-            return 0
-
-        lax.fori_loop(0, 9, w_step2, 0)
-
-        def w_step3(t, _):
-            w_in(t, 2 * xi + 1 - c).wait_recv()
-            w_in(t, 2 * (1 - xi) + 1 - c).wait_recv()
-            return 0
-
-        lax.fori_loop(0, 9, w_step3, 0)
-
         def g_in(j, b):
             return remote(ge.at[b, j + 1, pl.ds(PAD, R), :], ge.at[b, j + 1, pl.ds(PAD, R), :], s_gf.at[j], s_gr.at[b, j], y_dev)
 
@@ -163,10 +134,59 @@
             relay_in(j).wait_recv()
             relay_out(j).start()
 
-        lax.fori_loop(0, AHEAD, lambda j, _: (g_relay(j), 0)[1], 0)
+        def relay_rows(lo, hi):
+            lax.fori_loop(lo, min(hi, H), lambda j, _: (g_relay(j), 0)[1], 0)
+
+        tp_x = 2 * (1 - xi) + c
+        left_dev = (jnp.maximum(zi - 1, 0), st, tp)
+        right_dev = (jnp.minimum(zi + 1, 3), st, tp)
+
+        def w_unit(b, q, send_sem, dev):
+            view = wall.at[b, :, pl.ds(pl.multiple_of(q * quarter, quarter), quarter), :]
+            return remote(view, view, send_sem, s_wr.at[b, q], dev)
+
+        def w_got(q, go_right, go_left):
+            w_unit(tp, q, s_ws.at[0, q], y_dev).wait_recv()
+            if go_right:
+                @pl.when(zi < 3)
+                def _():
+                    w_unit(tp, q, s_ws.at[2, q], right_dev).start()
+            if go_left:
+                @pl.when(zi > 0)
+                def _():
+                    w_unit(tp, q, s_ws.at[3, q], left_dev).start()
+            w_unit(tp, q, s_ws.at[0, q], x_dev).start()
+            w_unit(tp, q, s_ws.at[1, q], c_dev).start()
+
+        w_got(zi, True, True)
+        for d in range(1, 4):
+            @pl.when(zi - d >= 0)
+            def _():
+                w_got(zi - d, True, False)
+
+            @pl.when(zi + d <= 3)
+            def _():
+                w_got(zi + d, False, True)
+
+            relay_rows(3 * (d - 1), 3 * d)
+
+        def w_cross(q, _):
+            w_unit(tp_x, q, s_ws.at[4, q], x_dev).wait_recv()
+            w_unit(tp_x, q, s_ws.at[4, q], c_dev).start()
+            return 0
+
+        lax.fori_loop(0, 4, w_cross, 0)
+
+        def w_all(q, _):
+            for b in (2 * xi + 1 - c, 2 * (1 - xi) + 1 - c):
+                w_unit(b, q, s_ws.at[1, q], c_dev).wait_recv()
+            return 0
+
+        lax.fori_loop(0, 4, w_all, 0)
+        relay_rows(9, 9 + AHEAD)
 
         def g_step(j, _):
-            @pl.when(j + AHEAD < H)
+            @pl.when(jnp.logical_and(j + AHEAD >= min(9 + AHEAD, H), j + AHEAD < H))
             def _():
                 g_relay(j + AHEAD)
 
@@ -260,13 +280,22 @@
 
         lax.fori_loop(0, H, drain, 0)
 
-        def drain_w(t, _):
-            w_fwd(t, tp, 0, c_dev).wait_send()
-            w_fwd(t, tp, 1, x_dev).wait_send()
-            w_fwd(t, b_x, 2, c_dev).wait_send()
-            return 0
-
-        lax.fori_loop(0, 9, drain_w, 0)
+        def drain_w(q, _):
+            w_unit(tp, q, s_ws.at[0, q], x_dev).wait_send()
+            w_unit(tp, q, s_ws.at[1, q], c_dev).wait_send()
+            w_unit(tp_x, q, s_ws.at[4, q], c_dev).wait_send()
+
+            @pl.when(jnp.logical_and(zi < 3, q <= zi))
+            def _():
+                w_unit(tp, q, s_ws.at[2, q], right_dev).wait_send()
+
+            @pl.when(jnp.logical_and(zi > 0, q >= zi))
+            def _():
+                w_unit(tp, q, s_ws.at[3, q], left_dev).wait_send()
+
+            return 0
+
+        lax.fori_loop(0, 4, drain_w, 0)
 
     @pl.when(st == 1)
     def _():
@@ -277,9 +306,10 @@
         dz_l = [pltpu.make_async_copy(dz_ref.at[:, :, 2 * s + c], dzb.at[s, c], s_dl.at[s]) for s in range(2)]
         dz_r = [remote(dz_ref.at[:, :, 2 * s + 1 - c], dzb.at[s, c], s_ds.at[s], s_dr.at[s], c_dev) for s in range(2)]
 
-        def w_y(t):
-            return remote(w_ref.at[t], wall.at[tp, t], s_ws.at[0, t], s_wr.at[tp, t], y_dev)
-
+        part = pl.ds(pl.multiple_of(zi * quarter, quarter), quarter)
+        w_y = remote(w_ref.at[:, part, :], wall.at[tp, :, part, :], s_ws.at[0, zi], s_wr.at[tp, zi], y_dev)
+
+        w_y.start()
         w_loc.start()
         w_core.start()
         for k in range(2):
@@ -287,7 +317,6 @@
             vecs_r[k].start()
             dz_l[k].start()
             dz_r[k].start()
-        lax.fori_loop(0, 9, lambda t, _: (w_y(t).start(), 0)[1], 0)
 
         zero_borders(xe)
         zero_borders(ge)
@@ -487,12 +516,12 @@
         lax.fori_loop(0, H, drain, 0)
 
         def drain_w(t, _):
-            w_y(t).wait_send()
             pair(t).wait_send()
             return 0
 
         lax.fori_loop(0, 9, drain_w, 0)
         w_core.wait_send()
+        w_y.wait_send()
         for k in range(2):
             vecs_r[k].wait_send()
             dz_r[k].wait_send()
@@ -562,7 +591,7 @@
                 pltpu.VMEM((CI, 256), BF16),
                 pltpu.VMEM((H, R, 2 * CO), BF16),
                 dma((H,)), dma((2, H)), dma((H,)), dma((2, H)), dma((2, H)), dma((H,)), dma((H,)),
-                dma, dma((3, 9)), dma((4, 9)), dma((2,)), dma((3,)), dma((3,)), dma((2,)), dma((2,)), dma((2,)),
+                dma, dma((5, 4)), dma((4, 4)), dma((2,)), dma((3,)), dma((3,)), dma((2,)), dma((2,)), dma((2,)),
                 dma((2,)), dma((2,)), dma((9,)), dma((9,)),
                 *[dma((n_chunk,))] * 10,
             ],

time: 107 us -> 116 us (1.084)
  Pallas kernels: 105 us -> 114 us
    pallas_call x1, Pallas kernels: 102 us -> 112 us  [device_step(): pl.pallas_call(functools.partial(block_kernel, H, WD, CI, CO, n_chunk), o...]
where the time goes in v5:
time: 116 us; the launch traced here: 115 us
  Pallas kernels  114 us (98%)
    pallas_call x1, Pallas kernels, device_step(): pl.pallas_call(functools.partial(block_kernel, H, WD, CI, CO, n_chunk), o...  112 us
    pallas_call x1, Pallas kernels, write_out(): pl.pallas_call(out_kernel, out_shape=tuple((jax.ShapeDtypeStruct(a.shape,...  2.49 us

profile of v5, /device:TPU:4, one launch (start us, length us, event | category | flops | bytes accessed | tf_op | source)
XLA Modules:
  0.0 115.0 jit_solution(641290352498249862)
XLA Ops:
  0.6 111.9 %shard_map.76 = (bf16[14,14,4,8,128]{4,3,2,1,0:T(8,128)(2,1)S(1)}, bf16[14,112,512]{2,1,0:T(8,128)(2,1)S(1)}, f32[9,512,128]{2,1,0:T(8,128)S(1)}) custom-call(bf16[14,112,512]{2,1,0:T(8,128)(2,1)} %bitcast.22, bf16[9,512,128]{2,1,0:T(8,128)(2,1)} %bitcast.24, f32[1,128]{1,0:T(1,128)} %gam_ref.1, f32[1,128]{1,0:T(1,128)} %bet_ref.1, ...), custom_call_target="tpu_custom_call" | custom-call | tf_op jit(solution)/shard_map/pallas_call | solution.py:568
  112.5 2.5 %shard_map.77 = (bf16[14,14,4,8,128]{4,3,2,1,0:T(8,128)(2,1)}, bf16[14,112,512]{2,1,0:T(8,128)(2,1)}, f32[9,512,128]{2,1,0:T(8,128)}) custom-call(bf16[14,14,4,8,128]{4,3,2,1,0:T(8,128)(2,1)S(1)} %get-tuple-element.9.refs_0_, bf16[14,112,512]{2,1,0:T(8,128)(2,1)S(1)} %get-tuple-element.10.refs_1_, f32[9,512,128]{2,1,0:T(8,128)S(1)} %get-tuple-element.11.refs_2_), custom_call_target="tpu_custom_call" | custom-call | tf_op jit(solution)/shard_map/pallas_call | solution.py:542

commit v6 on v5

--- a/solution.py
+++ b/solution.py
@@ -12,8 +12,9 @@
 BF16 = jnp.bfloat16
 PAD = 16
 AHEAD = 2
-LAG = 2
-N_B = 8
+LAG = 3
+LAG_OUT = 8
+N_B = 16
 
 
 def remote(src, dst, send_sem, recv_sem, dev):
@@ -26,7 +27,8 @@
      s_zs, s_zr, s_ps, s_pr, s_os, s_or, s_ms, s_mr, s_ts, s_tr,
      s_bs, s_br, s_us, s_ur) = sems
     R = WD * 8
-    half = CI // 2
+    sub = n_chunk // 9
+    piece = CI // sub
     quarter = CI // 4
     n_a = n_chunk - N_B
     CW = 2 * CO
@@ -88,7 +90,7 @@
         return odd[s, plane, start:start + n, :]
 
     def dw_view(k):
-        return dw_ref.at[k // 2, pl.ds(pl.multiple_of((k % 2) * half, half), half), :]
+        return dw_ref.at[k // sub, pl.ds(pl.multiple_of((k % sub) * piece, piece), piece), :]
 
     def part_up(k):
         return remote(pb.at[k], pb.at[k], s_os.at[k], s_or.at[k], y_dev)
@@ -183,13 +185,9 @@
             return 0
 
         lax.fori_loop(0, 4, w_all, 0)
-        relay_rows(9, 9 + AHEAD)
-
-        def g_step(j, _):
-            @pl.when(jnp.logical_and(j + AHEAD >= min(9 + AHEAD, H), j + AHEAD < H))
-            def _():
-                g_relay(j + AHEAD)
-
+        relay_rows(9, H)
+
+        def g_step(j):
             @pl.when(j < H)
             def _():
                 g_in(j, xi).wait_recv()
@@ -210,68 +208,66 @@
                             tot = tot + lax.dot_general(lhs, rhs, (((1,), (1,)), ((), ())), preferred_element_type=F32)
                 dx_ref[h] = tot.astype(BF16)
 
-            return 0
-
-        lax.fori_loop(0, H + 1, g_step, 0)
-
         def b_to_inner(k, dev):
             return remote(pb.at[k], rb.at[k], s_bs.at[k], s_br.at[k], dev)
 
         def b_to_outer(k, dev):
             return remote(rb.at[k], mb.at[k], s_us.at[k], s_ur.at[k], dev)
 
-        @pl.when(jnp.logical_not(inner))
-        def _():
-            def up(k, _):
+        def b_step(i, _):
+            k = n_a + i
+
+            @pl.when(k < n_chunk)
+            def _():
                 part_up(k).wait_recv()
-                b_to_inner(k, inner_dev).start()
-                return 0
-
-            lax.fori_loop(n_a, n_chunk, up, 0)
-
-            def down(k, _):
-                b_to_outer(k, inner_dev).wait_recv()
-                total_down(mb, k).start()
-                return 0
-
-            lax.fori_loop(n_a, n_chunk, down, 0)
-
-            def done(k, _):
-                b_to_inner(k, inner_dev).wait_send()
-                total_down(mb, k).wait_send()
-                return 0
-
-            lax.fori_loop(n_a, n_chunk, done, 0)
-
-        @pl.when(inner)
-        def _():
-            def both(k, _):
-                @pl.when(k < n_chunk)
+
+                @pl.when(jnp.logical_not(inner))
                 def _():
-                    part_up(k).wait_recv()
+                    b_to_inner(k, inner_dev).start()
+
+                @pl.when(inner)
+                def _():
                     b_to_inner(k, outer_dev).wait_recv()
                     pb[k] = pb[k] + rb[k]
                     to_mate(k).start()
 
-                @pl.when(k >= n_a + LAG)
-                def _():
-                    m = k - LAG
-                    to_mate(m).wait_recv()
-                    rb[m] = pb[m] + mb[m]
-                    b_to_outer(m, outer_dev).start()
-                    total_down(rb, m).start()
-
-                return 0
-
-            lax.fori_loop(n_a, n_chunk + LAG, both, 0)
-
-            def done(k, _):
+            @pl.when(jnp.logical_and(inner, jnp.logical_and(i >= LAG, k < n_chunk + LAG)))
+            def _():
+                m = k - LAG
+                to_mate(m).wait_recv()
+                rb[m] = pb[m] + mb[m]
+                b_to_outer(m, outer_dev).start()
+                total_down(rb, m).start()
+
+            @pl.when(jnp.logical_and(jnp.logical_not(inner), i >= LAG_OUT))
+            def _():
+                m = k - LAG_OUT
+                b_to_outer(m, inner_dev).wait_recv()
+                total_down(mb, m).start()
+
+            @pl.when(i <= H)
+            def _():
+                g_step(i)
+
+            return 0
+
+        lax.fori_loop(0, N_B + LAG_OUT, b_step, 0)
+
+        def b_done(k, _):
+            total_down(rb, k).wait_send()
+
+            @pl.when(jnp.logical_not(inner))
+            def _():
+                b_to_inner(k, inner_dev).wait_send()
+
+            @pl.when(inner)
+            def _():
                 to_mate(k).wait_send()
                 b_to_outer(k, outer_dev).wait_send()
-                total_down(rb, k).wait_send()
-                return 0
-
-            lax.fori_loop(n_a, n_chunk, done, 0)
+
+            return 0
+
+        lax.fori_loop(n_a, n_chunk, b_done, 0)
 
         def drain(h, _):
             x_copy(h).wait_send()
@@ -418,27 +414,27 @@
         def pair(t):
             return remote(acc.at[1 - c, t], prx.at[t], s_ps.at[t], s_pr.at[t], c_dev)
 
-        lax.fori_loop(0, 9, lambda i, _: (pair((i + n_a // 2) % 9).start(), 0)[1], 0)
+        lax.fori_loop(0, 9, lambda i, _: (pair((i + n_a // sub) % 9).start(), 0)[1], 0)
         z_r = [remote(zb.at[s, 1 - c], z_ref.at[:, :, 2 * s + c], s_zs.at[s], s_zr.at[s], c_dev) for s in range(2)]
         z_w = [remote(zb.at[s, 1 - c], z_ref.at[:, :, 2 * s + 1 - c], s_zs.at[s], s_zr.at[s], c_dev) for s in range(2)]
         for s in range(2):
             z_r[s].start()
 
         def own_part(k, fresh):
-            t = k // 2
-            q = pl.multiple_of((k % 2) * half, half)
+            t = k // sub
+            q = pl.multiple_of((k % sub) * piece, piece)
 
             @pl.when(fresh)
             def _():
                 pair(t).wait_recv()
 
-            return acc[c, t, pl.ds(q, half), :] + prx[t, pl.ds(q, half), :]
+            return acc[c, t, pl.ds(q, piece), :] + prx[t, pl.ds(q, piece), :]
 
         def part_a(k):
-            return own_part(k, jnp.logical_and(k % 2 == 0, k // 2 < n_a // 2))
+            return own_part(k, jnp.logical_and(k % sub == 0, k // sub < n_a // sub))
 
         def send_b(k, _):
-            pb[k] = own_part(k, jnp.logical_or(k % 2 == 0, k == n_a))
+            pb[k] = own_part(k, jnp.logical_or(k % sub == 0, k == n_a))
             part_up(k).start()
             return 0
 
@@ -486,7 +482,7 @@
                 def _():
                     m = k - LAG
                     to_mate(m).wait_recv()
-                    dw_ref[m // 2, pl.ds(pl.multiple_of((m % 2) * half, half), half), :] = pb[m] + mb[m]
+                    dw_ref[m // sub, pl.ds(pl.multiple_of((m % sub) * piece, piece), piece), :] = pb[m] + mb[m]
                     to_outer(m).start()
 
                 return 0
@@ -560,7 +556,7 @@
         CO = w_conv.shape[-1]
         R = WD * N
         RP = 128 + 2 * PAD
-        n_chunk = 18
+        n_chunk = 36
         x = act_in[0].transpose(1, 2, 0, 3).reshape(H, R, CI)
         w = w_conv[0].reshape(9, CI, CO)
         dz = z_grad[0].transpose(1, 2, 0, 3).reshape(H, WD, 4, N, CO)
@@ -585,9 +581,9 @@
                 pltpu.VMEM((2, 2, 1, CO), F32),
                 pltpu.VMEM((2, 9, CI, CO), F32),
                 pltpu.VMEM((9, CI, CO), F32),
-                pltpu.VMEM((n_chunk, CI // 2, CO), F32),
-                pltpu.VMEM((n_chunk, CI // 2, CO), F32),
-                pltpu.VMEM((n_chunk, CI // 2, CO), F32),
+                pltpu.VMEM((n_chunk, CI // 4, CO), F32),
+                pltpu.VMEM((n_chunk, CI // 4, CO), F32),
+                pltpu.VMEM((n_chunk, CI // 4, CO), F32),
                 pltpu.VMEM((CI, 256), BF16),
                 pltpu.VMEM((H, R, 2 * CO), BF16),
                 dma((H,)), dma((2, H)), dma((H,)), dma((2, H)), dma((2, H)), dma((H,)), dma((H,)),

time: 116 us -> 99.8 us (0.86)
  Pallas kernels: 114 us -> 98.4 us
    pallas_call x1, Pallas kernels: 112 us -> 95.9 us  [device_step(): pl.pallas_call(functools.partial(block_kernel, H, WD, CI, CO, n_chunk), o...]
where the time goes in v6:
time: 99.8 us; the launch traced here: 99 us
  Pallas kernels  98.4 us (99%)
    pallas_call x1, Pallas kernels, device_step(): pl.pallas_call(functools.partial(block_kernel, H, WD, CI, CO, n_chunk), o...  95.9 us
    pallas_call x1, Pallas kernels, write_out(): pl.pallas_call(out_kernel, out_shape=tuple((jax.ShapeDtypeStruct(a.shape,...  2.49 us

profile of v6, /device:TPU:4, one launch (start us, length us, event | category | flops | bytes accessed | tf_op | source)
XLA Modules:
  0.0 99.0 jit_solution(1433727295055739429)
XLA Ops:
  0.6 95.9 %shard_map.76 = (bf16[14,14,4,8,128]{4,3,2,1,0:T(8,128)(2,1)S(1)}, bf16[14,112,512]{2,1,0:T(8,128)(2,1)S(1)}, f32[9,512,128]{2,1,0:T(8,128)S(1)}) custom-call(bf16[14,112,512]{2,1,0:T(8,128)(2,1)} %bitcast.22, bf16[9,512,128]{2,1,0:T(8,128)(2,1)} %bitcast.24, f32[1,128]{1,0:T(1,128)} %gam_ref.1, f32[1,128]{1,0:T(1,128)} %bet_ref.1, ...), custom_call_target="tpu_custom_call" | custom-call | tf_op jit(solution)/shard_map/pallas_call | solution.py:564
  96.5 2.5 %shard_map.77 = (bf16[14,14,4,8,128]{4,3,2,1,0:T(8,128)(2,1)}, bf16[14,112,512]{2,1,0:T(8,128)(2,1)}, f32[9,512,128]{2,1,0:T(8,128)}) custom-call(bf16[14,14,4,8,128]{4,3,2,1,0:T(8,128)(2,1)S(1)} %get-tuple-element.9.refs_0_, bf16[14,112,512]{2,1,0:T(8,128)(2,1)S(1)} %get-tuple-element.10.refs_1_, f32[9,512,128]{2,1,0:T(8,128)S(1)} %get-tuple-element.11.refs_2_), custom_call_target="tpu_custom_call" | custom-call | tf_op jit(solution)/shard_map/pallas_call | solution.py:538

commit v7 on v6

--- a/solution.py
+++ b/solution.py
@@ -89,6 +89,11 @@
         start = PAD + 8 * shift - 8
         return odd[s, plane, start:start + n, :]
 
+    x_cut = ((0, R // 2 // 16 * 16), (R // 2 // 16 * 16, R - R // 2 // 16 * 16))
+
+    def x_view(s, h, p):
+        return xe.at[s, h + 1, pl.ds(PAD + x_cut[p][0], x_cut[p][1]), :]
+
     def dw_view(k):
         return dw_ref.at[k // sub, pl.ds(pl.multiple_of((k % sub) * piece, piece), piece), :]
 
@@ -103,10 +108,15 @@
 
     @pl.when(st == 0)
     def _():
-        def x_copy(h):
-            return remote(x_ref.at[h], xe.at[xi, h + 1, pl.ds(PAD, R), :], s_xs.at[h], s_xr.at[xi, h], y_dev)
-
-        lax.fori_loop(0, H, lambda h, _: (x_copy(h).start(), 0)[1], 0)
+        def x_copy(h, p):
+            return remote(x_ref.at[h, pl.ds(*x_cut[p]), :], x_view(xi, h, p), s_xs.at[p, h], s_xr.at[xi, p, h], y_dev)
+
+        def x_send(h, _):
+            for p in range(2):
+                x_copy(h, p).start()
+            return 0
+
+        lax.fori_loop(0, H, x_send, 0)
         zero_borders(ge)
         zero_planes(ge)
         zero_planes(go)
@@ -170,7 +180,10 @@
             def _():
                 w_got(zi + d, False, True)
 
-            relay_rows(3 * (d - 1), 3 * d)
+            if d > 1:
+                relay_rows(3 * (d - 2), 3 * (d - 1))
+
+        relay_rows(6, 8)
 
         def w_cross(q, _):
             w_unit(tp_x, q, s_ws.at[4, q], x_dev).wait_recv()
@@ -178,6 +191,7 @@
             return 0
 
         lax.fori_loop(0, 4, w_cross, 0)
+        relay_rows(8, H)
 
         def w_all(q, _):
             for b in (2 * xi + 1 - c, 2 * (1 - xi) + 1 - c):
@@ -185,7 +199,6 @@
             return 0
 
         lax.fori_loop(0, 4, w_all, 0)
-        relay_rows(9, H)
 
         def g_step(j):
             @pl.when(j < H)
@@ -270,7 +283,8 @@
         lax.fori_loop(n_a, n_chunk, b_done, 0)
 
         def drain(h, _):
-            x_copy(h).wait_send()
+            for p in range(2):
+                x_copy(h, p).wait_send()
             relay_out(h).wait_send()
             return 0
 
@@ -339,13 +353,11 @@
         w_loc.wait()
         w_core.wait_recv()
 
-        def x_in(j, s):
-            view = xe.at[s, j + 1, pl.ds(PAD, R), :]
-            return remote(view, view, s_xf.at[j], s_xr.at[s, j], y_dev)
-
-        def x_fwd(j):
-            view = xe.at[xi, j + 1, pl.ds(PAD, R), :]
-            return remote(view, view, s_xf.at[j], s_xr.at[xi, j], x_dev)
+        def x_in(j, s, p):
+            return remote(x_view(s, j, p), x_view(s, j, p), s_xf.at[p, j], s_xr.at[s, p, j], y_dev)
+
+        def x_fwd(j, p):
+            return remote(x_view(xi, j, p), x_view(xi, j, p), s_xf.at[p, j], s_xr.at[xi, p, j], x_dev)
 
         def g_own(h):
             return remote(ge.at[xi, h + 1, pl.ds(PAD, R), :], ge.at[xi, h + 1, pl.ds(PAD, R), :], s_gs.at[0, h], s_gr.at[xi, h], y_dev)
@@ -354,10 +366,21 @@
             return remote(ge.at[1 - xi, h + 1, pl.ds(PAD, R), :], relay.at[h], s_gs.at[1, h], s_gl.at[h], y_dev)
 
         def x_relay(j):
-            x_in(j, xi).wait_recv()
-            x_fwd(j).start()
+            for p in range(2):
+                x_in(j, xi, p).wait_recv()
+                x_fwd(j, p).start()
 
         lax.fori_loop(0, AHEAD, lambda j, _: (x_relay(j), 0)[1], 0)
+
+        def turn_x(q):
+            rows = jnp.concatenate([xe[s, q + 1, PAD:PAD + 128, :] for s in range(2)], axis=0)
+            xt[...] = rows.T
+
+        def add_dw(q, t):
+            rhs = jnp.concatenate([tap_rows(ge, go, s, q + 2 - t // 3, 1 - t % 3, 128) for s in range(2)], axis=0)
+            prod = jnp.dot(xt[...], rhs, preferred_element_type=F32)
+            for k in range(2):
+                acc[k, t] += prod[:, k * CO:(k + 1) * CO]
 
         def step(j, _):
             @pl.when(j + AHEAD < H)
@@ -366,7 +389,8 @@
 
             @pl.when(j < H)
             def _():
-                x_in(j, 1 - xi).wait_recv()
+                for p in range(2):
+                    x_in(j, 1 - xi, p).wait_recv()
                 for s in range(2):
                     odd_copy(xe, xo, s, j + 1)
 
@@ -396,25 +420,24 @@
 
             @pl.when(j >= 2)
             def _():
-                q = j - 2
-                rows = jnp.concatenate([xe[s, q + 1, PAD:PAD + 128, :] for s in range(2)], axis=0)
-                xt[...] = rows.T
-                for ky in range(3):
-                    for kx in range(3):
-                        t = 3 * ky + kx
-                        rhs = jnp.concatenate([tap_rows(ge, go, s, q + 2 - ky, 1 - kx, 128) for s in range(2)], axis=0)
-                        part = jnp.dot(xt[...], rhs, preferred_element_type=F32)
-                        for k in range(2):
-                            acc[k, t] += part[:, k * CO:(k + 1) * CO]
-
-            return 0
-
-        lax.fori_loop(0, H + 2, step, 0)
+                turn_x(j - 2)
+                for t in range(9):
+                    add_dw(j - 2, t)
+
+            return 0
+
+        lax.fori_loop(0, H + 1, step, 0)
 
         def pair(t):
             return remote(acc.at[1 - c, t], prx.at[t], s_ps.at[t], s_pr.at[t], c_dev)
 
-        lax.fori_loop(0, 9, lambda i, _: (pair((i + n_a // sub) % 9).start(), 0)[1], 0)
+        n_t = n_a // sub
+        order = sorted(range(9), key=lambda t: 2 * (t - n_t) if t >= n_t else 2 * t + 1)
+        turn_x(H - 1)
+        for t in order:
+            if t >= 3:
+                add_dw(H - 1, t)
+            pair(t).start()
         z_r = [remote(zb.at[s, 1 - c], z_ref.at[:, :, 2 * s + c], s_zs.at[s], s_zr.at[s], c_dev) for s in range(2)]
         z_w = [remote(zb.at[s, 1 - c], z_ref.at[:, :, 2 * s + 1 - c], s_zs.at[s], s_zr.at[s], c_dev) for s in range(2)]
         for s in range(2):
@@ -433,12 +456,12 @@
         def part_a(k):
             return own_part(k, jnp.logical_and(k % sub == 0, k // sub < n_a // sub))
 
-        def send_b(k, _):
-            pb[k] = own_part(k, jnp.logical_or(k % sub == 0, k == n_a))
-            part_up(k).start()
-            return 0
-
-        lax.fori_loop(n_a, n_chunk, send_b, 0)
+        def send_b(i):
+            @pl.when(i < N_B)
+            def _():
+                k = n_a + i
+                pb[k] = own_part(k, jnp.logical_or(k % sub == 0, k == n_a))
+                part_up(k).start()
 
         def to_inner(k):
             return remote(pb.at[k], rb.at[k], s_os.at[k], s_or.at[k], inner_dev)
@@ -455,11 +478,16 @@
         @pl.when(jnp.logical_not(inner))
         def _():
             def send(k, _):
-                pb[k] = part_a(k)
-                to_inner(k).start()
+                send_b(k)
+
+                @pl.when(k < n_a)
+                def _():
+                    pb[k] = part_a(k)
+                    to_inner(k).start()
+
                 return 0
 
-            lax.fori_loop(0, n_a, send, 0)
+            lax.fori_loop(0, max(n_a, N_B), send, 0)
 
             def take(k, _):
                 from_inner(k).wait_recv()
@@ -471,6 +499,9 @@
         @pl.when(inner)
         def _():
             def both(k, _):
+                for i in range(2):
+                    send_b(2 * k + i)
+
                 @pl.when(k < n_a)
                 def _():
                     part = part_a(k)
@@ -504,7 +535,8 @@
         lax.fori_loop(n_a, n_chunk, done_b, 0)
 
         def drain(h, _):
-            x_fwd(h).wait_send()
+            for p in range(2):
+                x_fwd(h, p).wait_send()
             g_own(h).wait_send()
             g_other(h).wait_send()
             return 0
@@ -586,7 +618,7 @@
                 pltpu.VMEM((n_chunk, CI // 4, CO), F32),
                 pltpu.VMEM((CI, 256), BF16),
                 pltpu.VMEM((H, R, 2 * CO), BF16),
-                dma((H,)), dma((2, H)), dma((H,)), dma((2, H)), dma((2, H)), dma((H,)), dma((H,)),
+                dma((2, H)), dma((2, 2, H)), dma((2, H)), dma((2, H)), dma((2, H)), dma((H,)), dma((H,)),
                 dma, dma((5, 4)), dma((4, 4)), dma((2,)), dma((3,)), dma((3,)), dma((2,)), dma((2,)), dma((2,)),
                 dma((2,)), dma((2,)), dma((9,)), dma((9,)),
                 *[dma((n_chunk,))] * 10,

time: 99.8 us -> 101 us (1.012)
  Pallas kernels: 98.4 us -> 99.5 us
    pallas_call x1, Pallas kernels: 95.9 us -> 97 us  [device_step(): pl.pallas_call(functools.partial(block_kernel, H, WD, CI, CO, n_chunk), o...]
where the time goes in v7:
time: 101 us; the launch traced here: 100 us
  Pallas kernels  99.5 us (99%)
    pallas_call x1, Pallas kernels, device_step(): pl.pallas_call(functools.partial(block_kernel, H, WD, CI, CO, n_chunk), o...  97 us
    pallas_call x1, Pallas kernels, write_out(): pl.pallas_call(out_kernel, out_shape=tuple((jax.ShapeDtypeStruct(a.shape,...  2.49 us

profile of v7, /device:TPU:4, one launch (start us, length us, event | category | flops | bytes accessed | tf_op | source)
XLA Modules:
  0.0 100.2 jit_solution(5416731697449743782)
XLA Ops:
  0.6 97.0 %shard_map.76 = (bf16[14,14,4,8,128]{4,3,2,1,0:T(8,128)(2,1)S(1)}, bf16[14,112,512]{2,1,0:T(8,128)(2,1)S(1)}, f32[9,512,128]{2,1,0:T(8,128)S(1)}) custom-call(bf16[14,112,512]{2,1,0:T(8,128)(2,1)} %bitcast.22, bf16[9,512,128]{2,1,0:T(8,128)(2,1)} %bitcast.24, f32[1,128]{1,0:T(1,128)} %gam_ref.1, f32[1,128]{1,0:T(1,128)} %bet_ref.1, ...), custom_call_target="tpu_custom_call" | custom-call | tf_op jit(solution)/shard_map/pallas_call | solution.py:596
  97.7 2.5 %shard_map.77 = (bf16[14,14,4,8,128]{4,3,2,1,0:T(8,128)(2,1)}, bf16[14,112,512]{2,1,0:T(8,128)(2,1)}, f32[9,512,128]{2,1,0:T(8,128)}) custom-call(bf16[14,14,4,8,128]{4,3,2,1,0:T(8,128)(2,1)S(1)} %get-tuple-element.9.refs_0_, bf16[14,112,512]{2,1,0:T(8,128)(2,1)S(1)} %get-tuple-element.10.refs_1_, f32[9,512,128]{2,1,0:T(8,128)S(1)} %get-tuple-element.11.refs_2_), custom_call_target="tpu_custom_call" | custom-call | tf_op jit(solution)/shard_map/pallas_call | solution.py:570

commit v8 on v7

--- a/solution.py
+++ b/solution.py
@@ -12,9 +12,9 @@
 BF16 = jnp.bfloat16
 PAD = 16
 AHEAD = 2
-LAG = 3
-LAG_OUT = 8
-N_B = 16
+LAG = 5
+LAG_OUT = 14
+N_B = 30
 
 
 def remote(src, dst, send_sem, recv_sem, dev):
@@ -24,12 +24,12 @@
 def block_kernel(H, WD, CI, CO, n_chunk, x_ref, w_ref, gam_ref, bet_ref, dz_ref, z_ref, dx_ref, dw_ref,
                  xe, xo, ge, go, wall, dzb, zb, vec, acc, prx, pb, rb, mb, xt, relay, *sems):
     (s_xs, s_xr, s_xf, s_gs, s_gr, s_gl, s_gf, s_wl, s_ws, s_wr, s_vl, s_vs, s_vr, s_dl, s_ds, s_dr,
-     s_zs, s_zr, s_ps, s_pr, s_os, s_or, s_ms, s_mr, s_ts, s_tr,
-     s_bs, s_br, s_us, s_ur) = sems
+     s_zs, s_zr, s_ps, s_pr, s_os, s_or, s_ms, s_mr, s_ts, s_tr) = sems
     R = WD * 8
     sub = n_chunk // 9
     piece = CI // sub
     quarter = CI // 4
+    n_blk = min(CI, 256)
     n_a = n_chunk - N_B
     CW = 2 * CO
     zi = lax.axis_index("dp")
@@ -153,22 +153,26 @@
         left_dev = (jnp.maximum(zi - 1, 0), st, tp)
         right_dev = (jnp.minimum(zi + 1, 3), st, tp)
 
-        def w_unit(b, q, send_sem, dev):
-            view = wall.at[b, :, pl.ds(pl.multiple_of(q * quarter, quarter), quarter), :]
-            return remote(view, view, send_sem, s_wr.at[b, q], dev)
+        def w_unit(b, q, y, kind, dev):
+            view = wall.at[b, pl.ds(3 * y, 3), pl.ds(pl.multiple_of(q * quarter, quarter), quarter), :]
+            return remote(view, view, s_ws.at[kind, q, y], s_wr.at[b, q, y], dev)
 
         def w_got(q, go_right, go_left):
-            w_unit(tp, q, s_ws.at[0, q], y_dev).wait_recv()
-            if go_right:
-                @pl.when(zi < 3)
-                def _():
-                    w_unit(tp, q, s_ws.at[2, q], right_dev).start()
-            if go_left:
-                @pl.when(zi > 0)
-                def _():
-                    w_unit(tp, q, s_ws.at[3, q], left_dev).start()
-            w_unit(tp, q, s_ws.at[0, q], x_dev).start()
-            w_unit(tp, q, s_ws.at[1, q], c_dev).start()
+            def take(y, _):
+                w_unit(tp, q, y, 0, y_dev).wait_recv()
+                if go_right:
+                    @pl.when(zi < 3)
+                    def _():
+                        w_unit(tp, q, y, 2, right_dev).start()
+                if go_left:
+                    @pl.when(zi > 0)
+                    def _():
+                        w_unit(tp, q, y, 3, left_dev).start()
+                w_unit(tp, q, y, 0, x_dev).start()
+                w_unit(tp, q, y, 1, c_dev).start()
+                return 0
+
+            lax.fori_loop(0, 3, take, 0)
 
         w_got(zi, True, True)
         for d in range(1, 4):
@@ -180,52 +184,63 @@
             def _():
                 w_got(zi + d, False, True)
 
-            if d > 1:
-                relay_rows(3 * (d - 2), 3 * (d - 1))
-
-        relay_rows(6, 8)
+            relay_rows(2 * (d - 1), 2 * d)
 
         def w_cross(q, _):
-            w_unit(tp_x, q, s_ws.at[4, q], x_dev).wait_recv()
-            w_unit(tp_x, q, s_ws.at[4, q], c_dev).start()
+            for y in range(3):
+                w_unit(tp_x, q, y, 4, x_dev).wait_recv()
+                w_unit(tp_x, q, y, 4, c_dev).start()
             return 0
 
         lax.fori_loop(0, 4, w_cross, 0)
-        relay_rows(8, H)
+        relay_rows(6, 10)
 
         def w_all(q, _):
-            for b in (2 * xi + 1 - c, 2 * (1 - xi) + 1 - c):
-                w_unit(b, q, s_ws.at[1, q], c_dev).wait_recv()
+            for y in range(3):
+                for b in (2 * xi + 1 - c, 2 * (1 - xi) + 1 - c):
+                    w_unit(b, q, y, 1, c_dev).wait_recv()
             return 0
 
         lax.fori_loop(0, 4, w_all, 0)
 
-        def g_step(j):
-            @pl.when(j < H)
-            def _():
-                g_in(j, xi).wait_recv()
-                g_in(j, 1 - xi).wait_recv()
+        G = 4
+
+        def g_take(j, _):
+            g_in(j, xi).wait_recv()
+            g_in(j, 1 - xi).wait_recv()
+            for b in range(2):
+                odd_copy(ge, go, b, j + 1)
+            return 0
+
+        def dx_rows(h0):
+            for n in range(CI // n_blk):
+                tot = jnp.zeros((G * R, n_blk), F32)
                 for b in range(2):
-                    odd_copy(ge, go, b, j + 1)
-
-            @pl.when(j >= 1)
-            def _():
-                h = j - 1
-                tot = jnp.zeros((R, CI), F32)
-                for b in range(2):
-                    for ky in range(3):
-                        for kx in range(3):
-                            t = 3 * ky + kx
-                            lhs = tap_rows(ge, go, b, h + 2 - ky, 1 - kx, R)
-                            rhs = jnp.concatenate([wall[2 * b, t], wall[2 * b + 1, t]], axis=1)
-                            tot = tot + lax.dot_general(lhs, rhs, (((1,), (1,)), ((), ())), preferred_element_type=F32)
-                dx_ref[h] = tot.astype(BF16)
+                    for t in range(9):
+                        lhs = jnp.concatenate([tap_rows(ge, go, b, h0 + r + 2 - t // 3, 1 - t % 3, R) for r in range(G)], axis=0)
+                        rhs = jnp.concatenate([wall[2 * b + i, t, n * n_blk:(n + 1) * n_blk, :] for i in range(2)], axis=1)
+                        tot = tot + lax.dot_general(lhs, rhs, (((1,), (1,)), ((), ())), preferred_element_type=F32)
+                for r in range(G):
+                    dx_ref[h0 + r, :, n * n_blk:(n + 1) * n_blk] = tot[r * R:(r + 1) * R].astype(BF16)
+
+        def dx_step(i, _):
+            lo = jnp.where(i == 0, 0, G * i + 1)
+            hi = jnp.minimum(G * i + G + 1, H)
+            @pl.when(i >= 1)
+            def _():
+                lax.fori_loop(jnp.minimum(8 + 2 * i, H), jnp.minimum(10 + 2 * i, H), lambda j, _: (g_relay(j), 0)[1], 0)
+
+            lax.fori_loop(lo, hi, g_take, 0)
+            dx_rows(jnp.minimum(G * i, H - G))
+            return 0
+
+        lax.fori_loop(0, -(-H // G), dx_step, 0)
 
         def b_to_inner(k, dev):
-            return remote(pb.at[k], rb.at[k], s_bs.at[k], s_br.at[k], dev)
+            return remote(pb.at[k], rb.at[k], s_os.at[k], s_tr.at[k], dev)
 
         def b_to_outer(k, dev):
-            return remote(rb.at[k], mb.at[k], s_us.at[k], s_ur.at[k], dev)
+            return remote(rb.at[k], mb.at[k], s_os.at[k], s_mr.at[k], dev)
 
         def b_step(i, _):
             k = n_a + i
@@ -252,15 +267,11 @@
                 b_to_outer(m, outer_dev).start()
                 total_down(rb, m).start()
 
-            @pl.when(jnp.logical_and(jnp.logical_not(inner), i >= LAG_OUT))
+            @pl.when(jnp.logical_and(jnp.logical_not(inner), jnp.logical_and(i >= LAG_OUT, i < N_B + LAG_OUT)))
             def _():
                 m = k - LAG_OUT
                 b_to_outer(m, inner_dev).wait_recv()
                 total_down(mb, m).start()
-
-            @pl.when(i <= H)
-            def _():
-                g_step(i)
 
             return 0
 
@@ -291,17 +302,18 @@
         lax.fori_loop(0, H, drain, 0)
 
         def drain_w(q, _):
-            w_unit(tp, q, s_ws.at[0, q], x_dev).wait_send()
-            w_unit(tp, q, s_ws.at[1, q], c_dev).wait_send()
-            w_unit(tp_x, q, s_ws.at[4, q], c_dev).wait_send()
-
-            @pl.when(jnp.logical_and(zi < 3, q <= zi))
-            def _():
-                w_unit(tp, q, s_ws.at[2, q], right_dev).wait_send()
-
-            @pl.when(jnp.logical_and(zi > 0, q >= zi))
-            def _():
-                w_unit(tp, q, s_ws.at[3, q], left_dev).wait_send()
+            for y in range(3):
+                w_unit(tp, q, y, 0, x_dev).wait_send()
+                w_unit(tp, q, y, 1, c_dev).wait_send()
+                w_unit(tp_x, q, y, 4, c_dev).wait_send()
+
+                @pl.when(jnp.logical_and(zi < 3, q <= zi))
+                def _():
+                    w_unit(tp, q, y, 2, right_dev).wait_send()
+
+                @pl.when(jnp.logical_and(zi > 0, q >= zi))
+                def _():
+                    w_unit(tp, q, y, 3, left_dev).wait_send()
 
             return 0
 
@@ -317,9 +329,10 @@
         dz_r = [remote(dz_ref.at[:, :, 2 * s + 1 - c], dzb.at[s, c], s_ds.at[s], s_dr.at[s], c_dev) for s in range(2)]
 
         part = pl.ds(pl.multiple_of(zi * quarter, quarter), quarter)
-        w_y = remote(w_ref.at[:, part, :], wall.at[tp, :, part, :], s_ws.at[0, zi], s_wr.at[tp, zi], y_dev)
-
-        w_y.start()
+        w_y = [remote(w_ref.at[3 * y:3 * y + 3, part, :], wall.at[tp, 3 * y:3 * y + 3, part, :], s_ws.at[0, zi, y], s_wr.at[tp, zi, y], y_dev) for y in range(3)]
+
+        for y in range(3):
+            w_y[y].start()
         w_loc.start()
         w_core.start()
         for k in range(2):
@@ -549,7 +562,8 @@
 
         lax.fori_loop(0, 9, drain_w, 0)
         w_core.wait_send()
-        w_y.wait_send()
+        for y in range(3):
+            w_y[y].wait_send()
         for k in range(2):
             vecs_r[k].wait_send()
             dz_r[k].wait_send()
@@ -588,7 +602,7 @@
         CO = w_conv.shape[-1]
         R = WD * N
         RP = 128 + 2 * PAD
-        n_chunk = 36
+        n_chunk = 72
         x = act_in[0].transpose(1, 2, 0, 3).reshape(H, R, CI)
         w = w_conv[0].reshape(9, CI, CO)
         dz = z_grad[0].transpose(1, 2, 0, 3).reshape(H, WD, 4, N, CO)
@@ -613,15 +627,15 @@
                 pltpu.VMEM((2, 2, 1, CO), F32),
                 pltpu.VMEM((2, 9, CI, CO), F32),
                 pltpu.VMEM((9, CI, CO), F32),
-                pltpu.VMEM((n_chunk, CI // 4, CO), F32),
-                pltpu.VMEM((n_chunk, CI // 4, CO), F32),
-                pltpu.VMEM((n_chunk, CI // 4, CO), F32),
+                pltpu.VMEM((n_chunk, CI // 8, CO), F32),
+                pltpu.VMEM((n_chunk, CI // 8, CO), F32),
+                pltpu.VMEM((n_chunk, CI // 8, CO), F32),
                 pltpu.VMEM((CI, 256), BF16),
                 pltpu.VMEM((H, R, 2 * CO), BF16),
                 dma((2, H)), dma((2, 2, H)), dma((2, H)), dma((2, H)), dma((2, H)), dma((H,)), dma((H,)),
-                dma, dma((5, 4)), dma((4, 4)), dma((2,)), dma((3,)), dma((3,)), dma((2,)), dma((2,)), dma((2,)),
+                dma, dma((5, 4, 3)), dma((4, 4, 3)), dma((2,)), dma((3,)), dma((3,)), dma((2,)), dma((2,)), dma((2,)),
                 dma((2,)), dma((2,)), dma((9,)), dma((9,)),
-                *[dma((n_chunk,))] * 10,
+                *[dma((n_chunk,))] * 6,
             ],
             compiler_params=pltpu.CompilerParams(collective_id=0, has_side_effects=True, vmem_limit_bytes=46 * 1024 * 1024),
         )(*[pltpu.with_memory_space_constraint(a, pltpu.HBM) for a in (x, w, gamma_vec, beta_vec, dz)])

time: 101 us -> 101 us (level)
  no operation moved by 1% of the time
where the time goes in v8:
time: 101 us; the launch traced here: 100 us
  Pallas kernels  99.7 us (99%)
    pallas_call x1, Pallas kernels, device_step(): pl.pallas_call(functools.partial(block_kernel, H, WD, CI, CO, n_chunk), o...  97.2 us
    pallas_call x1, Pallas kernels, write_out(): pl.pallas_call(out_kernel, out_shape=tuple((jax.ShapeDtypeStruct(a.shape,...  2.49 us

profile of v8, /device:TPU:4, one launch (start us, length us, event | category | flops | bytes accessed | tf_op | source)
XLA Modules:
  0.0 100.4 jit_solution(13935399072131049690)
XLA Ops:
  0.6 97.2 %shard_map.76 = (bf16[14,14,4,8,128]{4,3,2,1,0:T(8,128)(2,1)S(1)}, bf16[14,112,512]{2,1,0:T(8,128)(2,1)S(1)}, f32[9,512,128]{2,1,0:T(8,128)S(1)}) custom-call(bf16[14,112,512]{2,1,0:T(8,128)(2,1)} %bitcast.22, bf16[9,512,128]{2,1,0:T(8,128)(2,1)} %bitcast.24, f32[1,128]{1,0:T(1,128)} %gam_ref.1, f32[1,128]{1,0:T(1,128)} %bet_ref.1, ...), custom_call_target="tpu_custom_call" | custom-call | tf_op jit(solution)/shard_map/pallas_call | solution.py:610
  97.9 2.5 %shard_map.77 = (bf16[14,14,4,8,128]{4,3,2,1,0:T(8,128)(2,1)}, bf16[14,112,512]{2,1,0:T(8,128)(2,1)}, f32[9,512,128]{2,1,0:T(8,128)}) custom-call(bf16[14,14,4,8,128]{4,3,2,1,0:T(8,128)(2,1)S(1)} %get-tuple-element.9.refs_0_, bf16[14,112,512]{2,1,0:T(8,128)(2,1)S(1)} %get-tuple-element.10.refs_1_, f32[9,512,128]{2,1,0:T(8,128)S(1)} %get-tuple-element.11.refs_2_), custom_call_target="tpu_custom_call" | custom-call | tf_op jit(solution)/shard_map/pallas_call | solution.py:584

commit v9 on v8

--- a/solution.py
+++ b/solution.py
@@ -12,25 +12,25 @@
 BF16 = jnp.bfloat16
 PAD = 16
 AHEAD = 2
-LAG = 5
-LAG_OUT = 14
-N_B = 30
+LAG = 1
+LAG_OUT = 3
+CHUNKS_A = ((0, 0, 1), (0, 1, 1), (0, 2, 2), (1, 0, 4), (2, 0, 4), (3, 0, 4), (4, 0, 2), (4, 2, 1), (4, 3, 1))
+CHUNKS_B = ((5, 0, 1), (5, 1, 1), (5, 2, 2), (6, 0, 4), (7, 0, 4), (8, 0, 2), (8, 2, 1), (8, 3, 1))
+CHUNKS = CHUNKS_A + CHUNKS_B
+N_A, N_B = len(CHUNKS_A), len(CHUNKS_B)
 
 
 def remote(src, dst, send_sem, recv_sem, dev):
     return pltpu.make_async_remote_copy(src_ref=src, dst_ref=dst, send_sem=send_sem, recv_sem=recv_sem, device_id=dev, device_id_type=MESH)
 
 
-def block_kernel(H, WD, CI, CO, n_chunk, x_ref, w_ref, gam_ref, bet_ref, dz_ref, z_ref, dx_ref, dw_ref,
+def block_kernel(H, WD, CI, CO, x_ref, w_ref, gam_ref, bet_ref, dz_ref, z_ref, dx_ref, dw_ref,
                  xe, xo, ge, go, wall, dzb, zb, vec, acc, prx, pb, rb, mb, xt, relay, *sems):
     (s_xs, s_xr, s_xf, s_gs, s_gr, s_gl, s_gf, s_wl, s_ws, s_wr, s_vl, s_vs, s_vr, s_dl, s_ds, s_dr,
      s_zs, s_zr, s_ps, s_pr, s_os, s_or, s_ms, s_mr, s_ts, s_tr) = sems
     R = WD * 8
-    sub = n_chunk // 9
-    piece = CI // sub
     quarter = CI // 4
     n_blk = min(CI, 256)
-    n_a = n_chunk - N_B
     CW = 2 * CO
     zi = lax.axis_index("dp")
     st = lax.axis_index("stage")
@@ -89,22 +89,35 @@
         start = PAD + 8 * shift - 8
         return odd[s, plane, start:start + n, :]
 
-    x_cut = ((0, R // 2 // 16 * 16), (R // 2 // 16 * 16, R - R // 2 // 16 * 16))
+    x_cut = ((0, R),)
 
     def x_view(s, h, p):
         return xe.at[s, h + 1, pl.ds(PAD + x_cut[p][0], x_cut[p][1]), :]
 
-    def dw_view(k):
-        return dw_ref.at[k // sub, pl.ds(pl.multiple_of((k % sub) * piece, piece), piece), :]
+    def place(k):
+        t, q0, nq = CHUNKS[k]
+        return t, slice(q0 * quarter, (q0 + nq) * quarter)
+
+    def cut(buf, k):
+        t, rows = place(k)
+        return buf.at[t, rows, :]
+
+    def value(buf, k):
+        t, rows = place(k)
+        return buf[t, rows, :]
+
+    def put(buf, k, val):
+        t, rows = place(k)
+        buf[t, rows, :] = val
 
     def part_up(k):
-        return remote(pb.at[k], pb.at[k], s_os.at[k], s_or.at[k], y_dev)
+        return remote(cut(pb, k), cut(pb, k), s_os.at[k], s_or.at[k], y_dev)
 
     def to_mate(k):
-        return remote(pb.at[k], mb.at[k], s_ms.at[k], s_mr.at[k], mate_dev)
+        return remote(cut(pb, k), cut(mb, k), s_ms.at[k], s_mr.at[k], mate_dev)
 
     def total_down(src, k):
-        return remote(src.at[k], dw_view(k), s_ts.at[k], s_tr.at[k], y_dev)
+        return remote(cut(src, k), cut(dw_ref, k), s_ts.at[k], s_tr.at[k], y_dev)
 
     @pl.when(st == 0)
     def _():
@@ -112,7 +125,7 @@
             return remote(x_ref.at[h, pl.ds(*x_cut[p]), :], x_view(xi, h, p), s_xs.at[p, h], s_xr.at[xi, p, h], y_dev)
 
         def x_send(h, _):
-            for p in range(2):
+            for p in range(len(x_cut)):
                 x_copy(h, p).start()
             return 0
 
@@ -134,17 +147,18 @@
         lax.fori_loop(0, 9, zero_dw, 0)
 
         def g_in(j, b):
-            return remote(ge.at[b, j + 1, pl.ds(PAD, R), :], ge.at[b, j + 1, pl.ds(PAD, R), :], s_gf.at[j], s_gr.at[b, j], y_dev)
+            return remote(ge.at[b, j + 1, pl.ds(PAD, R), :], ge.at[b, j + 1, pl.ds(PAD, R), :], s_gf.at[j], s_gr.at[b, j], x_dev)
 
         def relay_in(j):
-            return remote(relay.at[j], relay.at[j], s_gf.at[j], s_gl.at[j], y_dev)
+            return remote(relay.at[:, j], relay.at[:, j], s_gf.at[j], s_gl.at[j], y_dev)
 
         def relay_out(j):
-            return remote(relay.at[j], ge.at[xi, j + 1, pl.ds(PAD, R), :], s_gf.at[j], s_gr.at[xi, j], x_dev)
+            return remote(relay.at[1 - xi, j], ge.at[xi, j + 1, pl.ds(PAD, R), :], s_gf.at[j], s_gr.at[xi, j], x_dev)
 
         def g_relay(j):
             relay_in(j).wait_recv()
             relay_out(j).start()
+            ge[xi, j + 1, PAD:PAD + R, :] = relay[xi, j]
 
         def relay_rows(lo, hi):
             lax.fori_loop(lo, min(hi, H), lambda j, _: (g_relay(j), 0)[1], 0)
@@ -192,8 +206,9 @@
                 w_unit(tp_x, q, y, 4, c_dev).start()
             return 0
 
+        relay_rows(6, 9)
         lax.fori_loop(0, 4, w_cross, 0)
-        relay_rows(6, 10)
+        relay_rows(9, H)
 
         def w_all(q, _):
             for y in range(3):
@@ -206,7 +221,6 @@
         G = 4
 
         def g_take(j, _):
-            g_in(j, xi).wait_recv()
             g_in(j, 1 - xi).wait_recv()
             for b in range(2):
                 odd_copy(ge, go, b, j + 1)
@@ -223,61 +237,89 @@
                 for r in range(G):
                     dx_ref[h0 + r, :, n * n_blk:(n + 1) * n_blk] = tot[r * R:(r + 1) * R].astype(BF16)
 
-        def dx_step(i, _):
-            lo = jnp.where(i == 0, 0, G * i + 1)
-            hi = jnp.minimum(G * i + G + 1, H)
-            @pl.when(i >= 1)
-            def _():
-                lax.fori_loop(jnp.minimum(8 + 2 * i, H), jnp.minimum(10 + 2 * i, H), lambda j, _: (g_relay(j), 0)[1], 0)
-
-            lax.fori_loop(lo, hi, g_take, 0)
-            dx_rows(jnp.minimum(G * i, H - G))
-            return 0
-
-        lax.fori_loop(0, -(-H // G), dx_step, 0)
+        def dx_step(i):
+            @pl.when(i >= 0)
+            def _():
+                lo = jnp.where(i == 0, 0, G * i + 1)
+                lax.fori_loop(lo, jnp.minimum(G * i + G + 1, H), g_take, 0)
+                dx_rows(jnp.minimum(G * i, H - G))
 
         def b_to_inner(k, dev):
-            return remote(pb.at[k], rb.at[k], s_os.at[k], s_tr.at[k], dev)
+            return remote(cut(pb, k), cut(rb, k), s_os.at[k], s_tr.at[k], dev)
 
         def b_to_outer(k, dev):
-            return remote(rb.at[k], mb.at[k], s_os.at[k], s_mr.at[k], dev)
-
-        def b_step(i, _):
-            k = n_a + i
-
-            @pl.when(k < n_chunk)
-            def _():
-                part_up(k).wait_recv()
+            return remote(cut(rb, k), cut(mb, k), s_os.at[k], s_mr.at[k], dev)
+
+        def b_up(k):
+            part_up(k).wait_recv()
+
+            @pl.when(jnp.logical_not(inner))
+            def _():
+                b_to_inner(k, inner_dev).start()
+
+            @pl.when(inner)
+            def _():
+                b_to_inner(k, outer_dev).wait_recv()
+                put(pb, k, value(pb, k) + value(rb, k))
+                to_mate(k).start()
+
+        def b_total(k):
+            to_mate(k).wait_recv()
+            put(rb, k, value(pb, k) + value(mb, k))
+            b_to_outer(k, outer_dev).start()
+            total_down(rb, k).start()
+
+        def b_down(k):
+            b_to_outer(k, inner_dev).wait_recv()
+            total_down(mb, k).start()
+
+        n_g = -(-H // G)
+        slots = N_A + N_B
+
+        def dx_loop(lo, hi):
+            lax.fori_loop(min(lo, n_g), min(hi, n_g), lambda i, _: (dx_step(i), 0)[1], 0)
+
+        def b_some(lo, hi):
+            for k in range(lo, hi):
+                b_up(k)
+
+                @pl.when(inner)
+                def _():
+                    if k - LAG >= N_A:
+                        b_total(k - LAG)
 
                 @pl.when(jnp.logical_not(inner))
                 def _():
-                    b_to_inner(k, inner_dev).start()
-
-                @pl.when(inner)
+                    if k - LAG_OUT >= N_A:
+                        b_down(k - LAG_OUT)
+
+        b_some(N_A, N_A + 3)
+
+        def dx_between(i, _):
+            for m in range(3):
+                @pl.when(i == m)
                 def _():
-                    b_to_inner(k, outer_dev).wait_recv()
-                    pb[k] = pb[k] + rb[k]
-                    to_mate(k).start()
-
-            @pl.when(jnp.logical_and(inner, jnp.logical_and(i >= LAG, k < n_chunk + LAG)))
-            def _():
-                m = k - LAG
-                to_mate(m).wait_recv()
-                rb[m] = pb[m] + mb[m]
-                b_to_outer(m, outer_dev).start()
-                total_down(rb, m).start()
-
-            @pl.when(jnp.logical_and(jnp.logical_not(inner), jnp.logical_and(i >= LAG_OUT, i < N_B + LAG_OUT)))
-            def _():
-                m = k - LAG_OUT
-                b_to_outer(m, inner_dev).wait_recv()
-                total_down(mb, m).start()
-
-            return 0
-
-        lax.fori_loop(0, N_B + LAG_OUT, b_step, 0)
-
-        def b_done(k, _):
+                    b_some(N_A + 3 + m, N_A + 4 + m)
+
+            dx_step(i)
+            return 0
+
+        lax.fori_loop(0, n_g, dx_between, 0)
+        if n_g < 3:
+            b_some(N_A + 3 + n_g, N_A + 6)
+        b_some(N_A + 6, slots)
+
+        @pl.when(inner)
+        def _():
+            for k in range(slots - LAG, slots):
+                b_total(k)
+
+        @pl.when(jnp.logical_not(inner))
+        def _():
+            for k in range(slots - LAG_OUT, slots):
+                b_down(k)
+
+        for k in range(N_A, slots):
             total_down(rb, k).wait_send()
 
             @pl.when(jnp.logical_not(inner))
@@ -289,12 +331,8 @@
                 to_mate(k).wait_send()
                 b_to_outer(k, outer_dev).wait_send()
 
-            return 0
-
-        lax.fori_loop(n_a, n_chunk, b_done, 0)
-
         def drain(h, _):
-            for p in range(2):
+            for p in range(len(x_cut)):
                 x_copy(h, p).wait_send()
             relay_out(h).wait_send()
             return 0
@@ -372,14 +410,11 @@
         def x_fwd(j, p):
             return remote(x_view(xi, j, p), x_view(xi, j, p), s_xf.at[p, j], s_xr.at[xi, p, j], x_dev)
 
-        def g_own(h):
-            return remote(ge.at[xi, h + 1, pl.ds(PAD, R), :], ge.at[xi, h + 1, pl.ds(PAD, R), :], s_gs.at[0, h], s_gr.at[xi, h], y_dev)
-
-        def g_other(h):
-            return remote(ge.at[1 - xi, h + 1, pl.ds(PAD, R), :], relay.at[h], s_gs.at[1, h], s_gl.at[h], y_dev)
+        def g_send(h):
+            return remote(ge.at[:, h + 1, pl.ds(PAD, R), :], relay.at[:, h], s_gs.at[h], s_gl.at[h], y_dev)
 
         def x_relay(j):
-            for p in range(2):
+            for p in range(len(x_cut)):
                 x_in(j, xi, p).wait_recv()
                 x_fwd(j, p).start()
 
@@ -402,7 +437,7 @@
 
             @pl.when(j < H)
             def _():
-                for p in range(2):
+                for p in range(len(x_cut)):
                     x_in(j, 1 - xi, p).wait_recv()
                 for s in range(2):
                     odd_copy(xe, xo, s, j + 1)
@@ -425,8 +460,7 @@
                         zb[s, k, h] = jnp.maximum(y, 0.0).reshape(WD, 8, CO).astype(BF16)
                         dzr = dzb[s, k, h].astype(F32).reshape(R, CO)
                         ge[s, h + 1, PAD:PAD + R, k * CO:(k + 1) * CO] = jnp.where(y > 0, dzr * gam, 0.0).astype(BF16)
-                g_own(h).start()
-                g_other(h).start()
+                g_send(h).start()
                 for s in range(2):
                     odd_copy(ge, go, s, h + 1)
                     z_ref[h, :, 2 * s + c] = zb[s, c, h]
@@ -444,7 +478,7 @@
         def pair(t):
             return remote(acc.at[1 - c, t], prx.at[t], s_ps.at[t], s_pr.at[t], c_dev)
 
-        n_t = n_a // sub
+        n_t = CHUNKS_B[0][0]
         order = sorted(range(9), key=lambda t: 2 * (t - n_t) if t >= n_t else 2 * t + 1)
         turn_x(H - 1)
         for t in order:
@@ -456,102 +490,67 @@
         for s in range(2):
             z_r[s].start()
 
-        def own_part(k, fresh):
-            t = k // sub
-            q = pl.multiple_of((k % sub) * piece, piece)
-
-            @pl.when(fresh)
-            def _():
+        def own_part(k):
+            t, rows = place(k)
+            if rows.start == 0:
                 pair(t).wait_recv()
-
-            return acc[c, t, pl.ds(q, piece), :] + prx[t, pl.ds(q, piece), :]
-
-        def part_a(k):
-            return own_part(k, jnp.logical_and(k % sub == 0, k // sub < n_a // sub))
+            return acc[c, t, rows, :] + prx[t, rows, :]
 
         def send_b(i):
-            @pl.when(i < N_B)
-            def _():
-                k = n_a + i
-                pb[k] = own_part(k, jnp.logical_or(k % sub == 0, k == n_a))
-                part_up(k).start()
+            if i < N_B:
+                put(pb, N_A + i, own_part(N_A + i))
+                part_up(N_A + i).start()
 
         def to_inner(k):
-            return remote(pb.at[k], rb.at[k], s_os.at[k], s_or.at[k], inner_dev)
+            return remote(cut(pb, k), cut(rb, k), s_os.at[k], s_or.at[k], inner_dev)
 
         def from_outer(k):
-            return remote(pb.at[k], rb.at[k], s_os.at[k], s_or.at[k], outer_dev)
+            return remote(cut(pb, k), cut(rb, k), s_os.at[k], s_or.at[k], outer_dev)
 
         def to_outer(k):
-            return remote(dw_view(k), dw_view(k), s_ts.at[k], s_tr.at[k], outer_dev)
+            return remote(cut(dw_ref, k), cut(dw_ref, k), s_ts.at[k], s_tr.at[k], outer_dev)
 
         def from_inner(k):
-            return remote(dw_view(k), dw_view(k), s_ts.at[k], s_tr.at[k], inner_dev)
+            return remote(cut(dw_ref, k), cut(dw_ref, k), s_ts.at[k], s_tr.at[k], inner_dev)
 
         @pl.when(jnp.logical_not(inner))
         def _():
-            def send(k, _):
+            for k in range(max(N_A, N_B)):
                 send_b(k)
-
-                @pl.when(k < n_a)
-                def _():
-                    pb[k] = part_a(k)
+                if k < N_A:
+                    put(pb, k, own_part(k))
                     to_inner(k).start()
-
-                return 0
-
-            lax.fori_loop(0, max(n_a, N_B), send, 0)
-
-            def take(k, _):
+            for k in range(N_A):
                 from_inner(k).wait_recv()
                 to_inner(k).wait_send()
-                return 0
-
-            lax.fori_loop(0, n_a, take, 0)
 
         @pl.when(inner)
         def _():
-            def both(k, _):
-                for i in range(2):
-                    send_b(2 * k + i)
-
-                @pl.when(k < n_a)
-                def _():
-                    part = part_a(k)
+            send_b(0)
+            for k in range(max(N_A + LAG, N_B)):
+                send_b(k + 1)
+                if k < N_A:
+                    part = own_part(k)
                     from_outer(k).wait_recv()
-                    pb[k] = part + rb[k]
+                    put(pb, k, part + value(rb, k))
                     to_mate(k).start()
-
-                @pl.when(k >= LAG)
-                def _():
-                    m = k - LAG
+                m = k - LAG
+                if 0 <= m < N_A:
                     to_mate(m).wait_recv()
-                    dw_ref[m // sub, pl.ds(pl.multiple_of((m % sub) * piece, piece), piece), :] = pb[m] + mb[m]
+                    put(dw_ref, m, value(pb, m) + value(mb, m))
                     to_outer(m).start()
-
-                return 0
-
-            lax.fori_loop(0, n_a + LAG, both, 0)
-
-            def done(k, _):
+            for k in range(N_A):
                 to_mate(k).wait_send()
                 to_outer(k).wait_send()
-                return 0
-
-            lax.fori_loop(0, n_a, done, 0)
-
-        def done_b(k, _):
+
+        for k in range(N_A, N_A + N_B):
             total_down(rb, k).wait_recv()
             part_up(k).wait_send()
-            return 0
-
-        lax.fori_loop(n_a, n_chunk, done_b, 0)
 
         def drain(h, _):
-            for p in range(2):
+            for p in range(len(x_cut)):
                 x_fwd(h, p).wait_send()
-            g_own(h).wait_send()
-            g_other(h).wait_send()
+            g_send(h).wait_send()
             return 0
 
         lax.fori_loop(0, H, drain, 0)
@@ -602,13 +601,12 @@
         CO = w_conv.shape[-1]
         R = WD * N
         RP = 128 + 2 * PAD
-        n_chunk = 72
         x = act_in[0].transpose(1, 2, 0, 3).reshape(H, R, CI)
         w = w_conv[0].reshape(9, CI, CO)
         dz = z_grad[0].transpose(1, 2, 0, 3).reshape(H, WD, 4, N, CO)
         dma = pltpu.SemaphoreType.DMA
         z, dx, dw = pl.pallas_call(
-            functools.partial(block_kernel, H, WD, CI, CO, n_chunk),
+            functools.partial(block_kernel, H, WD, CI, CO),
             out_shape=(
                 jax.ShapeDtypeStruct((H, WD, 4, N, CO), BF16),
                 jax.ShapeDtypeStruct((H, R, CI), BF16),
@@ -627,15 +625,15 @@
                 pltpu.VMEM((2, 2, 1, CO), F32),
                 pltpu.VMEM((2, 9, CI, CO), F32),
                 pltpu.VMEM((9, CI, CO), F32),
-                pltpu.VMEM((n_chunk, CI // 8, CO), F32),
-                pltpu.VMEM((n_chunk, CI // 8, CO), F32),
-                pltpu.VMEM((n_chunk, CI // 8, CO), F32),
+                pltpu.VMEM((9, CI, CO), F32),
+                pltpu.VMEM((9, CI, CO), F32),
+                pltpu.VMEM((9, CI, CO), F32),
                 pltpu.VMEM((CI, 256), BF16),
-                pltpu.VMEM((H, R, 2 * CO), BF16),
-                dma((2, H)), dma((2, 2, H)), dma((2, H)), dma((2, H)), dma((2, H)), dma((H,)), dma((H,)),
+                pltpu.VMEM((2, H, R, 2 * CO), BF16),
+                dma((1, H)), dma((2, 1, H)), dma((1, H)), dma((H,)), dma((2, H)), dma((H,)), dma((H,)),
                 dma, dma((5, 4, 3)), dma((4, 4, 3)), dma((2,)), dma((3,)), dma((3,)), dma((2,)), dma((2,)), dma((2,)),
                 dma((2,)), dma((2,)), dma((9,)), dma((9,)),
-                *[dma((n_chunk,))] * 6,
+                *[dma((N_A + N_B,))] * 6,
             ],
             compiler_params=pltpu.CompilerParams(collective_id=0, has_side_effects=True, vmem_limit_bytes=46 * 1024 * 1024),
         )(*[pltpu.with_memory_space_constraint(a, pltpu.HBM) for a in (x, w, gamma_vec, beta_vec, dz)])

time: 101 us -> 107 us (1.059)
  Pallas kernels: 99.7 us -> 105 us
    pallas_call x1, Pallas kernels: 97.2 us -> 103 us  [device_step(): pl.pallas_call(functools.partial(block_kernel, H, WD, CI, CO), out_shape=...]
where the time goes in v9:
time: 107 us; the launch traced here: 106 us
  Pallas kernels  105 us (98%)
    pallas_call x1, Pallas kernels, device_step(): pl.pallas_call(functools.partial(block_kernel, H, WD, CI, CO), out_shape=...  103 us
    pallas_call x1, Pallas kernels, write_out(): pl.pallas_call(out_kernel, out_shape=tuple((jax.ShapeDtypeStruct(a.shape,...  2.49 us

profile of v9, /device:TPU:4, one launch (start us, length us, event | category | flops | bytes accessed | tf_op | source)
XLA Modules:
  0.0 106.1 jit_solution(16900459345873420218)
XLA Ops:
  0.6 102.9 %shard_map.76 = (bf16[14,14,4,8,128]{4,3,2,1,0:T(8,128)(2,1)S(1)}, bf16[14,112,512]{2,1,0:T(8,128)(2,1)S(1)}, f32[9,512,128]{2,1,0:T(8,128)S(1)}) custom-call(bf16[14,112,512]{2,1,0:T(8,128)(2,1)} %bitcast.22, bf16[9,512,128]{2,1,0:T(8,128)(2,1)} %bitcast.24, f32[1,128]{1,0:T(1,128)} %gam_ref.1, f32[1,128]{1,0:T(1,128)} %bet_ref.1, ...), custom_call_target="tpu_custom_call" | custom-call | tf_op jit(solution)/shard_map/pallas_call | solution.py:608
  103.6 2.5 %shard_map.77 = (bf16[14,14,4,8,128]{4,3,2,1,0:T(8,128)(2,1)}, bf16[14,112,512]{2,1,0:T(8,128)(2,1)}, f32[9,512,128]{2,1,0:T(8,128)}) custom-call(bf16[14,14,4,8,128]{4,3,2,1,0:T(8,128)(2,1)S(1)} %get-tuple-element.9.refs_0_, bf16[14,112,512]{2,1,0:T(8,128)(2,1)S(1)} %get-tuple-element.10.refs_1_, f32[9,512,128]{2,1,0:T(8,128)S(1)} %get-tuple-element.11.refs_2_), custom_call_target="tpu_custom_call" | custom-call | tf_op jit(solution)/shard_map/pallas_call | solution.py:583

commit v10 on v9

--- a/solution.py
+++ b/solution.py
@@ -12,12 +12,11 @@
 BF16 = jnp.bfloat16
 PAD = 16
 AHEAD = 2
-LAG = 1
-LAG_OUT = 3
-CHUNKS_A = ((0, 0, 1), (0, 1, 1), (0, 2, 2), (1, 0, 4), (2, 0, 4), (3, 0, 4), (4, 0, 2), (4, 2, 1), (4, 3, 1))
-CHUNKS_B = ((5, 0, 1), (5, 1, 1), (5, 2, 2), (6, 0, 4), (7, 0, 4), (8, 0, 2), (8, 2, 1), (8, 3, 1))
-CHUNKS = CHUNKS_A + CHUNKS_B
-N_A, N_B = len(CHUNKS_A), len(CHUNKS_B)
+LAG = 3
+LAG_OUT = 8
+N_B = 14
+CHUNKS = tuple((t, q, 1) for t in range(9) for q in range(4))
+N_A = len(CHUNKS) - N_B
 
 
 def remote(src, dst, send_sem, recv_sem, dev):
@@ -293,21 +292,19 @@
                     if k - LAG_OUT >= N_A:
                         b_down(k - LAG_OUT)
 
-        b_some(N_A, N_A + 3)
+        b_some(N_A, N_A + 2)
 
         def dx_between(i, _):
-            for m in range(3):
+            for m in range(n_g):
                 @pl.when(i == m)
                 def _():
-                    b_some(N_A + 3 + m, N_A + 4 + m)
+                    b_some(N_A + 2 + 2 * m, N_A + 4 + 2 * m)
 
             dx_step(i)
             return 0
 
         lax.fori_loop(0, n_g, dx_between, 0)
-        if n_g < 3:
-            b_some(N_A + 3 + n_g, N_A + 6)
-        b_some(N_A + 6, slots)
+        b_some(N_A + 2 + 2 * n_g, slots)
 
         @pl.when(inner)
         def _():
@@ -478,7 +475,7 @@
         def pair(t):
             return remote(acc.at[1 - c, t], prx.at[t], s_ps.at[t], s_pr.at[t], c_dev)
 
-        n_t = CHUNKS_B[0][0]
+        n_t = CHUNKS[N_A][0]
         order = sorted(range(9), key=lambda t: 2 * (t - n_t) if t >= n_t else 2 * t + 1)
         turn_x(H - 1)
         for t in order:
@@ -492,7 +489,7 @@
 
         def own_part(k):
             t, rows = place(k)
-            if rows.start == 0:
+            if k == N_A or (rows.start == 0 and (k > N_A or t < n_t)):
                 pair(t).wait_recv()
             return acc[c, t, rows, :] + prx[t, rows, :]
 

time: 107 us -> 97 us (0.907)
  Pallas kernels: 105 us -> 96.2 us
    pallas_call x1, Pallas kernels: 103 us -> 93.7 us  [device_step(): pl.pallas_call(functools.partial(block_kernel, H, WD, CI, CO), out_shape=...]
where the time goes in v10:
time: 97 us; the launch traced here: 96.8 us
  Pallas kernels  96.2 us (99%)
    pallas_call x1, Pallas kernels, device_step(): pl.pallas_call(functools.partial(block_kernel, H, WD, CI, CO), out_shape=...  93.7 us
    pallas_call x1, Pallas kernels, write_out(): pl.pallas_call(out_kernel, out_shape=tuple((jax.ShapeDtypeStruct(a.shape,...  2.49 us

profile of v10, /device:TPU:4, one launch (start us, length us, event | category | flops | bytes accessed | tf_op | source)
XLA Modules:
  0.0 96.8 jit_solution(6279680647676620419)
XLA Ops:
  0.6 93.7 %shard_map.76 = (bf16[14,14,4,8,128]{4,3,2,1,0:T(8,128)(2,1)S(1)}, bf16[14,112,512]{2,1,0:T(8,128)(2,1)S(1)}, f32[9,512,128]{2,1,0:T(8,128)S(1)}) custom-call(bf16[14,112,512]{2,1,0:T(8,128)(2,1)} %bitcast.22, bf16[9,512,128]{2,1,0:T(8,128)(2,1)} %bitcast.24, f32[1,128]{1,0:T(1,128)} %gam_ref.1, f32[1,128]{1,0:T(1,128)} %bet_ref.1, ...), custom_call_target="tpu_custom_call" | custom-call | tf_op jit(solution)/shard_map/pallas_call | solution.py:605
  94.3 2.5 %shard_map.77 = (bf16[14,14,4,8,128]{4,3,2,1,0:T(8,128)(2,1)}, bf16[14,112,512]{2,1,0:T(8,128)(2,1)}, f32[9,512,128]{2,1,0:T(8,128)}) custom-call(bf16[14,14,4,8,128]{4,3,2,1,0:T(8,128)(2,1)S(1)} %get-tuple-element.9.refs_0_, bf16[14,112,512]{2,1,0:T(8,128)(2,1)S(1)} %get-tuple-element.10.refs_1_, f32[9,512,128]{2,1,0:T(8,128)S(1)} %get-tuple-element.11.refs_2_), custom_call_target="tpu_custom_call" | custom-call | tf_op jit(solution)/shard_map/pallas_call | solution.py:580

commit v11 on v10

--- a/solution.py
+++ b/solution.py
@@ -12,10 +12,12 @@
 BF16 = jnp.bfloat16
 PAD = 16
 AHEAD = 2
-LAG = 3
-LAG_OUT = 8
-N_B = 14
-CHUNKS = tuple((t, q, 1) for t in range(9) for q in range(4))
+LAG = 5
+LAG_OUT = 14
+N_B = 28
+PIECES = 8
+STEPS = 4
+CHUNKS = tuple((t, q) for t in range(9) for q in range(PIECES))
 N_A = len(CHUNKS) - N_B
 
 
@@ -88,14 +90,14 @@
         start = PAD + 8 * shift - 8
         return odd[s, plane, start:start + n, :]
 
-    x_cut = ((0, R),)
+    x_cut = ((0, 48), (48, R - 48))
 
     def x_view(s, h, p):
         return xe.at[s, h + 1, pl.ds(PAD + x_cut[p][0], x_cut[p][1]), :]
 
     def place(k):
-        t, q0, nq = CHUNKS[k]
-        return t, slice(q0 * quarter, (q0 + nq) * quarter)
+        t, q = CHUNKS[k]
+        return t, slice(q * (CI // PIECES), (q + 1) * (CI // PIECES))
 
     def cut(buf, k):
         t, rows = place(k)
@@ -292,19 +294,19 @@
                     if k - LAG_OUT >= N_A:
                         b_down(k - LAG_OUT)
 
-        b_some(N_A, N_A + 2)
+        b_some(N_A, N_A + STEPS)
 
         def dx_between(i, _):
             for m in range(n_g):
                 @pl.when(i == m)
                 def _():
-                    b_some(N_A + 2 + 2 * m, N_A + 4 + 2 * m)
+                    b_some(N_A + STEPS * (m + 1), N_A + STEPS * (m + 2))
 
             dx_step(i)
             return 0
 
         lax.fori_loop(0, n_g, dx_between, 0)
-        b_some(N_A + 2 + 2 * n_g, slots)
+        b_some(N_A + STEPS * (n_g + 1), slots)
 
         @pl.when(inner)
         def _():
@@ -627,7 +629,7 @@
                 pltpu.VMEM((9, CI, CO), F32),
                 pltpu.VMEM((CI, 256), BF16),
                 pltpu.VMEM((2, H, R, 2 * CO), BF16),
-                dma((1, H)), dma((2, 1, H)), dma((1, H)), dma((H,)), dma((2, H)), dma((H,)), dma((H,)),
+                dma((2, H)), dma((2, 2, H)), dma((2, H)), dma((H,)), dma((2, H)), dma((H,)), dma((H,)),
                 dma, dma((5, 4, 3)), dma((4, 4, 3)), dma((2,)), dma((3,)), dma((3,)), dma((2,)), dma((2,)), dma((2,)),
                 dma((2,)), dma((2,)), dma((9,)), dma((9,)),
                 *[dma((N_A + N_B,))] * 6,

time: 97 us -> 97.7 us (level)
  no operation moved by 1% of the time
where the time goes in v11:
time: 97.7 us; the launch traced here: 97.5 us
  Pallas kernels  96.9 us (99%)
    pallas_call x1, Pallas kernels, device_step(): pl.pallas_call(functools.partial(block_kernel, H, WD, CI, CO), out_shape=...  94.4 us
    pallas_call x1, Pallas kernels, write_out(): pl.pallas_call(out_kernel, out_shape=tuple((jax.ShapeDtypeStruct(a.shape,...  2.49 us

profile of v11, /device:TPU:4, one launch (start us, length us, event | category | flops | bytes accessed | tf_op | source)
XLA Modules:
  0.0 97.5 jit_solution(6400381512434795510)
XLA Ops:
  0.6 94.4 %shard_map.76 = (bf16[14,14,4,8,128]{4,3,2,1,0:T(8,128)(2,1)S(1)}, bf16[14,112,512]{2,1,0:T(8,128)(2,1)S(1)}, f32[9,512,128]{2,1,0:T(8,128)S(1)}) custom-call(bf16[14,112,512]{2,1,0:T(8,128)(2,1)} %bitcast.22, bf16[9,512,128]{2,1,0:T(8,128)(2,1)} %bitcast.24, f32[1,128]{1,0:T(1,128)} %gam_ref.1, f32[1,128]{1,0:T(1,128)} %bet_ref.1, ...), custom_call_target="tpu_custom_call" | custom-call | tf_op jit(solution)/shard_map/pallas_call | solution.py:607
  95.0 2.5 %shard_map.77 = (bf16[14,14,4,8,128]{4,3,2,1,0:T(8,128)(2,1)}, bf16[14,112,512]{2,1,0:T(8,128)(2,1)}, f32[9,512,128]{2,1,0:T(8,128)}) custom-call(bf16[14,14,4,8,128]{4,3,2,1,0:T(8,128)(2,1)S(1)} %get-tuple-element.9.refs_0_, bf16[14,112,512]{2,1,0:T(8,128)(2,1)S(1)} %get-tuple-element.10.refs_1_, f32[9,512,128]{2,1,0:T(8,128)S(1)} %get-tuple-element.11.refs_2_), custom_call_target="tpu_custom_call" | custom-call | tf_op jit(solution)/shard_map/pallas_call | solution.py:582

commit v12 on v10

--- a/solution.py
+++ b/solution.py
@@ -417,13 +417,16 @@
 
         lax.fori_loop(0, AHEAD, lambda j, _: (x_relay(j), 0)[1], 0)
 
+        for plane in (0, H + 1):
+            xt[plane] = jnp.zeros(xt.shape[1:], BF16)
+
         def turn_x(q):
             rows = jnp.concatenate([xe[s, q + 1, PAD:PAD + 128, :] for s in range(2)], axis=0)
-            xt[...] = rows.T
-
-        def add_dw(q, t):
-            rhs = jnp.concatenate([tap_rows(ge, go, s, q + 2 - t // 3, 1 - t % 3, 128) for s in range(2)], axis=0)
-            prod = jnp.dot(xt[...], rhs, preferred_element_type=F32)
+            xt[q + 1] = rows.T
+
+        def add_dw(h, t):
+            rhs = jnp.concatenate([tap_rows(ge, go, s, h + 1, 1 - t % 3, 128) for s in range(2)], axis=0)
+            prod = jnp.dot(xt[h + t // 3], rhs, preferred_element_type=F32)
             for k in range(2):
                 acc[k, t] += prod[:, k * CO:(k + 1) * CO]
 
@@ -438,6 +441,7 @@
                     x_in(j, 1 - xi, p).wait_recv()
                 for s in range(2):
                     odd_copy(xe, xo, s, j + 1)
+                turn_x(j)
 
             @pl.when(jnp.logical_and(j >= 1, j < H + 1))
             def _():
@@ -462,11 +466,11 @@
                     odd_copy(ge, go, s, h + 1)
                     z_ref[h, :, 2 * s + c] = zb[s, c, h]
 
-            @pl.when(j >= 2)
-            def _():
-                turn_x(j - 2)
-                for t in range(9):
-                    add_dw(j - 2, t)
+            @pl.when(jnp.logical_and(j >= 1, j < H))
+            def _():
+                for kx in range(3):
+                    for ky in range(3):
+                        add_dw(j - 1, 3 * ky + kx)
 
             return 0
 
@@ -477,9 +481,8 @@
 
         n_t = CHUNKS[N_A][0]
         order = sorted(range(9), key=lambda t: 2 * (t - n_t) if t >= n_t else 2 * t + 1)
-        turn_x(H - 1)
         for t in order:
-            if t >= 3:
+            if t < 6:
                 add_dw(H - 1, t)
             pair(t).start()
         z_r = [remote(zb.at[s, 1 - c], z_ref.at[:, :, 2 * s + c], s_zs.at[s], s_zr.at[s], c_dev) for s in range(2)]
@@ -625,7 +628,7 @@
                 pltpu.VMEM((9, CI, CO), F32),
                 pltpu.VMEM((9, CI, CO), F32),
                 pltpu.VMEM((9, CI, CO), F32),
-                pltpu.VMEM((CI, 256), BF16),
+                pltpu.VMEM((H + 2, CI, 256), BF16),
                 pltpu.VMEM((2, H, R, 2 * CO), BF16),
                 dma((1, H)), dma((2, 1, H)), dma((1, H)), dma((H,)), dma((2, H)), dma((H,)), dma((H,)),
                 dma, dma((5, 4, 3)), dma((4, 4, 3)), dma((2,)), dma((3,)), dma((3,)), dma((2,)), dma((2,)), dma((2,)),

time: 97 us -> 96.3 us (level)
  no operation moved by 1% of the time
where the time goes in v12:
time: 96.3 us; the launch traced here: 96.1 us
  Pallas kernels  95.5 us (99%)
    pallas_call x1, Pallas kernels, device_step(): pl.pallas_call(functools.partial(block_kernel, H, WD, CI, CO), out_shape=...  93 us
    pallas_call x1, Pallas kernels, write_out(): pl.pallas_call(out_kernel, out_shape=tuple((jax.ShapeDtypeStruct(a.shape,...  2.49 us

profile of v12, /device:TPU:4, one launch (start us, length us, event | category | flops | bytes accessed | tf_op | source)
XLA Modules:
  0.0 96.1 jit_solution(5654196179771898948)
XLA Ops:
  0.6 93.0 %shard_map.76 = (bf16[14,14,4,8,128]{4,3,2,1,0:T(8,128)(2,1)S(1)}, bf16[14,112,512]{2,1,0:T(8,128)(2,1)S(1)}, f32[9,512,128]{2,1,0:T(8,128)S(1)}) custom-call(bf16[14,112,512]{2,1,0:T(8,128)(2,1)} %bitcast.22, bf16[9,512,128]{2,1,0:T(8,128)(2,1)} %bitcast.24, f32[1,128]{1,0:T(1,128)} %gam_ref.1, f32[1,128]{1,0:T(1,128)} %bet_ref.1, ...), custom_call_target="tpu_custom_call" | custom-call | tf_op jit(solution)/shard_map/pallas_call | solution.py:608
  93.6 2.5 %shard_map.77 = (bf16[14,14,4,8,128]{4,3,2,1,0:T(8,128)(2,1)}, bf16[14,112,512]{2,1,0:T(8,128)(2,1)}, f32[9,512,128]{2,1,0:T(8,128)}) custom-call(bf16[14,14,4,8,128]{4,3,2,1,0:T(8,128)(2,1)S(1)} %get-tuple-element.9.refs_0_, bf16[14,112,512]{2,1,0:T(8,128)(2,1)S(1)} %get-tuple-element.10.refs_1_, f32[9,512,128]{2,1,0:T(8,128)S(1)} %get-tuple-element.11.refs_2_), custom_call_target="tpu_custom_call" | custom-call | tf_op jit(solution)/shard_map/pallas_call | solution.py:583

commit v13 on v12

--- a/solution.py
+++ b/solution.py
@@ -88,7 +88,7 @@
         start = PAD + 8 * shift - 8
         return odd[s, plane, start:start + n, :]
 
-    x_cut = ((0, R),)
+    x_cut = ((0, 48), (48, R - 48))
 
     def x_view(s, h, p):
         return xe.at[s, h + 1, pl.ds(PAD + x_cut[p][0], x_cut[p][1]), :]
@@ -630,7 +630,7 @@
                 pltpu.VMEM((9, CI, CO), F32),
                 pltpu.VMEM((H + 2, CI, 256), BF16),
                 pltpu.VMEM((2, H, R, 2 * CO), BF16),
-                dma((1, H)), dma((2, 1, H)), dma((1, H)), dma((H,)), dma((2, H)), dma((H,)), dma((H,)),
+                dma((2, H)), dma((2, 2, H)), dma((2, H)), dma((H,)), dma((2, H)), dma((H,)), dma((H,)),
                 dma, dma((5, 4, 3)), dma((4, 4, 3)), dma((2,)), dma((3,)), dma((3,)), dma((2,)), dma((2,)), dma((2,)),
                 dma((2,)), dma((2,)), dma((9,)), dma((9,)),
                 *[dma((N_A + N_B,))] * 6,

time: 96.3 us -> 96.2 us (level)
  no operation moved by 1% of the time
where the time goes in v13:
time: 96.2 us; the launch traced here: 96.1 us
  Pallas kernels  95.4 us (99%)
    pallas_call x1, Pallas kernels, device_step(): pl.pallas_call(functools.partial(block_kernel, H, WD, CI, CO), out_shape=...  93 us
    pallas_call x1, Pallas kernels, write_out(): pl.pallas_call(out_kernel, out_shape=tuple((jax.ShapeDtypeStruct(a.shape,...  2.49 us

profile of v13, /device:TPU:4, one launch (start us, length us, event | category | flops | bytes accessed | tf_op | source)
XLA Modules:
  0.0 96.1 jit_solution(2768312907517845492)
XLA Ops:
  0.6 93.0 %shard_map.76 = (bf16[14,14,4,8,128]{4,3,2,1,0:T(8,128)(2,1)S(1)}, bf16[14,112,512]{2,1,0:T(8,128)(2,1)S(1)}, f32[9,512,128]{2,1,0:T(8,128)S(1)}) custom-call(bf16[14,112,512]{2,1,0:T(8,128)(2,1)} %bitcast.22, bf16[9,512,128]{2,1,0:T(8,128)(2,1)} %bitcast.24, f32[1,128]{1,0:T(1,128)} %gam_ref.1, f32[1,128]{1,0:T(1,128)} %bet_ref.1, ...), custom_call_target="tpu_custom_call" | custom-call | tf_op jit(solution)/shard_map/pallas_call | solution.py:608
  93.6 2.5 %shard_map.77 = (bf16[14,14,4,8,128]{4,3,2,1,0:T(8,128)(2,1)}, bf16[14,112,512]{2,1,0:T(8,128)(2,1)}, f32[9,512,128]{2,1,0:T(8,128)}) custom-call(bf16[14,14,4,8,128]{4,3,2,1,0:T(8,128)(2,1)S(1)} %get-tuple-element.9.refs_0_, bf16[14,112,512]{2,1,0:T(8,128)(2,1)S(1)} %get-tuple-element.10.refs_1_, f32[9,512,128]{2,1,0:T(8,128)S(1)} %get-tuple-element.11.refs_2_), custom_call_target="tpu_custom_call" | custom-call | tf_op jit(solution)/shard_map/pallas_call | solution.py:583
